TPU v7x, 8 devices: a whole 2x2x1 slice. The times are simulated.
8 devices in a mesh: dp: 2 (over z, y), tp: 4 (over x, core).
Axes of the slice: x: 2, y: 2, z: 1, core: 2. Of those that a mesh axis runs over, the one named last changes fastest.
Arguments:
- hidden_in: bfloat16 [512, 1024], P('dp'), parts along dimension 0
- k_cache: bfloat16 [512, 256, 8, 64], P('dp', None, 'tp'), parts along dimension 0
- v_cache: bfloat16 [512, 256, 8, 64], P('dp', None, 'tp'), parts along dimension 0
- seq_lens: int32 [512], P('dp'), parts along dimension 0
- chosen_experts: int32 [512, 8], P('dp'), parts along dimension 0
- g_attn: bfloat16 [1024], replicated
- w_q: bfloat16 [1024, 1024], P(None, 'tp')
- w_k: bfloat16 [1024, 512], P(None, 'tp')
- w_v: bfloat16 [1024, 512], P(None, 'tp')
- w_o: bfloat16 [1024, 1024], P('tp')
- g_moe: bfloat16 [1024], replicated
- w_router: bfloat16 [1024, 32], replicated
- w_gate: bfloat16 [32, 1024, 512], P(None, None, 'tp')
- w_up: bfloat16 [32, 1024, 512], P(None, None, 'tp')
- w_down: bfloat16 [32, 512, 1024], P(None, 'tp')
Outputs:
- output 1: bfloat16 [512, 1024], P('dp'), parts along dimension 0
- output 2: bfloat16 [512, 256, 8, 64], P('dp', None, 'tp'), parts along dimension 0
- output 3: bfloat16 [512, 256, 8, 64], P('dp', None, 'tp'), parts along dimension 0
There are 2 independent parts. A program takes and returns all parts, laid end to end along the dimension named above; an argument that names none is the same for every part.
All inputs are finite; a program needn't handle non-finite values.
Results may differ from a plain program's by a relative error of at most 0.00751233.
Values are sent between devices in bfloat16 or wider.
A program may use at most 1 GiB of HBM per device.

v0:
```python
import jax
import jax.numpy as jnp
from jax import lax
from jax.sharding import PartitionSpec as P

EPSILON = 1e-5
ROPE_THETA = 1000000.0
MASK_FILL = -1e30


def rms_norm(vector, gain_w):
    vector32 = vector.astype(jnp.float32)
    norm_scale = lax.rsqrt(jnp.mean(vector32 * vector32, axis=-1, keepdims=True) + EPSILON)
    return (vector32 * norm_scale * gain_w.astype(jnp.float32)).astype(jnp.bfloat16)


def rope_rotate(vector, cos_t, sin_t):
    half_dim = vector.shape[-1] // 2
    lead_half = vector[..., :half_dim]
    tail_half = vector[..., half_dim:]
    return jnp.concatenate([lead_half * cos_t - tail_half * sin_t, tail_half * cos_t + lead_half * sin_t], axis=-1)


def attention_part(hidden_in, k_cache, v_cache, seq_lens, g_attn, w_q, w_k, w_v):
    num_rows, num_slots, kv_heads, head_dim = k_cache.shape
    q_group = w_q.shape[1] // (head_dim * kv_heads)
    h_attn = rms_norm(hidden_in, g_attn)
    q_lin = jnp.dot(h_attn, w_q, preferred_element_type=jnp.float32).reshape(num_rows, kv_heads, q_group, head_dim)
    k_lin = jnp.dot(h_attn, w_k, preferred_element_type=jnp.float32).reshape(num_rows, kv_heads, head_dim)
    v_new = jnp.dot(h_attn, w_v, preferred_element_type=jnp.float32).reshape(num_rows, kv_heads, head_dim).astype(jnp.bfloat16)
    inv_freq = ROPE_THETA ** (-jnp.arange(0, head_dim, 2, dtype=jnp.float32) / head_dim)
    angles = seq_lens.astype(jnp.float32)[:, None] * inv_freq[None, :]
    cos_t = jnp.cos(angles)[:, None, :]
    sin_t = jnp.sin(angles)[:, None, :]
    q_rot = rope_rotate(q_lin, cos_t[:, :, None, :], sin_t[:, :, None, :]).astype(jnp.bfloat16)
    k_new = rope_rotate(k_lin, cos_t, sin_t).astype(jnp.bfloat16)
    slot_ids = jnp.arange(num_slots, dtype=jnp.int32)
    new_slot = (slot_ids[None, :] == seq_lens[:, None])[:, :, None, None]
    k_next = jnp.where(new_slot, k_new[:, None, :, :], k_cache)
    v_next = jnp.where(new_slot, v_new[:, None, :, :], v_cache)
    scores = jnp.einsum("bkgd,bskd->bkgs", q_rot, k_next, preferred_element_type=jnp.float32) * (head_dim ** -0.5)
    in_range = (slot_ids[None, :] <= seq_lens[:, None])[:, None, None, :]
    attn_weights = jax.nn.softmax(jnp.where(in_range, scores, MASK_FILL), axis=-1).astype(jnp.bfloat16)
    heads_out = jnp.einsum("bkgs,bskd->bkgd", attn_weights, v_next, preferred_element_type=jnp.float32)
    return heads_out.astype(jnp.bfloat16).reshape(num_rows, kv_heads * q_group * head_dim), k_next, v_next


def experts_part(hidden_mid, chosen_experts, g_moe, w_router, w_gate, w_up, w_down):
    num_experts = w_router.shape[1]
    h_moe = rms_norm(hidden_mid, g_moe)
    logits = jnp.dot(h_moe, w_router, preferred_element_type=jnp.float32)
    pick_mask = (chosen_experts[:, :, None] == jnp.arange(num_experts, dtype=jnp.int32)[None, None, :]).astype(jnp.float32)
    gate_probs = jax.nn.softmax(jnp.sum(pick_mask * logits[:, None, :], axis=-1), axis=-1)
    gate_mat = jnp.sum(gate_probs[:, :, None] * pick_mask, axis=1)
    up_gate = jnp.einsum("bd,edf->bef", h_moe, w_gate, preferred_element_type=jnp.float32)
    up_lin = jnp.einsum("bd,edf->bef", h_moe, w_up, preferred_element_type=jnp.float32)
    inner_act = (gate_mat[:, :, None] * jax.nn.silu(up_gate) * up_lin).astype(jnp.bfloat16)
    return jnp.einsum("bef,efd->bd", inner_act, w_down, preferred_element_type=jnp.float32)


def solution(mesh):
    cache_spec = P("dp", None, "tp", None)
    in_specs = (P("dp", None), cache_spec, cache_spec, P("dp"), P("dp", None), P(None), P(None, "tp"), P(None, "tp"), P(None, "tp"), P("tp", None), P(None), P(None, None), P(None, None, "tp"), P(None, None, "tp"), P(None, "tp", None))
    out_specs = (P("dp", None), cache_spec, cache_spec)

    def layer_shard(hidden_in, k_cache, v_cache, seq_lens, chosen_experts, g_attn, w_q, w_k, w_v, w_o, g_moe, w_router, w_gate, w_up, w_down):
        heads_out, k_next, v_next = attention_part(hidden_in, k_cache, v_cache, seq_lens, g_attn, w_q, w_k, w_v)
        attn_local = jnp.dot(heads_out, w_o, preferred_element_type=jnp.float32)
        attn_sum = lax.psum(attn_local, "tp")
        hidden_mid = (hidden_in.astype(jnp.float32) + attn_sum).astype(jnp.bfloat16)
        moe_local = experts_part(hidden_mid, chosen_experts, g_moe, w_router, w_gate, w_up, w_down)
        moe_sum = lax.psum(moe_local, "tp")
        hidden_out = (hidden_mid.astype(jnp.float32) + moe_sum).astype(jnp.bfloat16)
        return hidden_out, k_next, v_next

    return jax.shard_map(layer_shard, mesh=mesh, in_specs=in_specs, out_specs=out_specs, check_vma=False)
```

profile of v0, /device:TPU:0, one launch (start us, length us, event | category | flops | bytes accessed | tf_op | source)
XLA Modules:
  0.0 155.6 jit_solution(644848833630994081)
XLA Ops:
  7.2 0.0 all-reduce.3.cloned.1.call-start
  7.2 0.7 convert_element_type.58
  8.0 0.8 iota_compare_fusion.2
  8.8 1.2 fusion.6
  10.0 0.7 convert_element_type.56
  10.7 1.5 convolution_convert_fusion.1
  12.2 0.1 copy.47
  12.3 0.2 multiply_cosine_fusion
  12.5 0.1 copy.43
  12.6 0.1 copy.45
  12.7 1.5 fusion.27
  14.3 0.1 copy.46
  14.4 1.6 %fusion.29 = f32[256,256]{0,1:T(8,128)S(1)} fusion(bf16[1024,256]{1,0:T(8,128)(2,1)} %param.21, bf16[256,1024]{1,0:T(8,128)(2,1)} %param.15, f32[1024]{0:T(1024)S(1)} %convert_element_type.56, f32[256]{0:T(256)S(1)} %add_rsqrt_fusion.1), kind=kOutput, calls=%fused_computation.55 | convolution fusion | flops 135266304 | bytes 1315840 | tf_op jit(solution)/shard_map/dot_general | solution.py:28
  16.1 0.3 copy.50
  16.4 0.3 copy.49
  16.7 0.5 subtract_convert_fusion
  17.3 22.2 %broadcast_select_fusion.1 = (bf16[256,256,2,64]{1,3,2,0:T(8,128)(2,1)}, bf16[256,256,2,64]{1,3,2,0:T(8,128)(2,1)}) fusion(bf16[256,256,2,64]{1,3,2,0:T(8,128)(2,1)} %param.16, pred[256,256]{1,0:T(8,128)(4,1)S(1)} %get-tuple-element.16, bf16[256,2,64]{2,1,0:T(2,128)(2,1)S(1)} %copy.46, bf16[256,256,2,64]{1,3,2,0:T(8,128)(2,1)} %param.17, ...), kind=kLoop, calls=%fused_computation.2 | loop fusion | flops 16777216 | bytes 67305472 | tf_op jit(solution)/shard_map/jit(_where)/select_n | solution.py:39
  39.5 7.7 %fusion.38 = (f32[256,2,2]{2,1,0:T(2,128)S(1)}, f32[256,2,2,256]{3,2,1,0:T(2,128)S(1)}) fusion(bf16[256,256,2,64]{1,3,2,0:T(8,128)(2,1)} %get-tuple-element.11, pred[256,256]{1,0:T(8,128)(4,1)S(1)} %get-tuple-element.15, bf16[256,2,2,32]{3,2,1,0:T(2,128)(2,1)S(1)} %get-tuple-element.6, bf16[256,2,2,32]{3,2,1,0:T(2,128)(2,1)S(1)} %get-tuple-element.5), kind=kOutput, calls=%fused_computation.58 | convolution fusion | flops 34865408 | bytes 18026496 | tf_op jit(solution)/shard_map/sub | solution.py:43
  47.3 10.3 %convolution_convert_fusion = bf16[256,2,2,64]{3,2,1,0:T(2,128)(2,1)S(1)} fusion(bf16[256,256,2,64]{1,3,2,0:T(8,128)(2,1)} %get-tuple-element.12, f32[256,2,2,256]{3,2,1,0:T(2,128)S(1)} %get-tuple-element.18, f32[256,2,2]{2,1,0:T(2,128)S(1)} %get-tuple-element.17), kind=kOutput, calls=%fused_computation.16 | convolution fusion | flops 34144256 | bytes 17960960 | tf_op jit(solution)/shard_map/bkgs,bskd->bkgd/dot_general | solution.py:44
  57.6 0.2 copy.48
  57.8 1.4 fusion.41
  59.1 0.0 all-reduce.3.cloned.1.call-update
  59.1 0.2 all-reduce.5.cloned.1.call-start
  59.4 33.5 %all-reduce.3.cloned.1.call-done = f32[256,1024]{1,0:T(8,128)} async-done(((f32[256,1024]{1,0:T(8,128)}), f32[256,1024]{1,0:T(8,128)}) %all-reduce.3.cloned.1.call-update) | async-done | bytes 1048592 | tf_op jit(solution)/shard_map/psum | solution.py:69
  92.9 1.5 fusion.10
  94.4 0.3 fusion.34
  94.7 0.0 copy-done.2
  94.9 7.7 %fusion.16 = f32[256,32,128]{2,0,1:T(8,128)} fusion(bf16[32,1024,128]{2,1,0:T(8,128)(2,1)} %param.27, bf16[256,1024]{1,0:T(8,128)(2,1)S(1)} %get-tuple-element.4, f32[1024]{0:T(1024)S(1)} %convert_element_type.65, f32[256]{0:T(256)S(1)} %add_rsqrt_fusion), kind=kOutput, calls=%fused_computation.28 | convolution fusion | flops 2148532224 | bytes 13112320 | tf_op jit(solution)/shard_map/bd,edf->bef/dot_general | solution.py:55
  102.6 12.7 %fusion.4 = f32[256,1024]{1,0:T(8,128)} fusion(bf16[32,128,1024]{2,1,0:T(8,128)(2,1)} %param.29, f32[256,32,128]{2,0,1:T(8,128)} %fusion.16, bf16[32,1024,128]{2,1,0:T(8,128)(2,1)} %param.28, f32[256,32]{0,1:T(8,128)S(1)} %select_reduce_fusion, bf16[256,1024]{1,0:T(8,128)(2,1)S(1)} %get-tuple-element.4, f32[1024]{0:T(1024)S(1)} %convert_element_type.65, ...), kind=kOutput, calls=%fused_computation.13 | convolution fusion | flops 4303355904 | bytes 22582272 | tf_op jit(solution)/shard_map/bef,efd->bd/dot_general | solution.py:58
  115.4 0.0 all-reduce.5.cloned.1.call-update
  115.4 31.3 %all-reduce.5.cloned.1.call-done = f32[256,1024]{1,0:T(8,128)} async-done(((f32[256,1024]{1,0:T(8,128)}), f32[256,1024]{1,0:T(8,128)}) %all-reduce.5.cloned.1.call-update) | async-done | bytes 1048592 | tf_op jit(solution)/shard_map/psum | solution.py:72
  146.6 2.2 %fusion.13 = bf16[256,1024]{1,0:T(8,128)(2,1)} fusion(f32[256,1024]{1,0:T(8,128)} %all-reduce.5.cloned.1.call-done, bf16[256,1024]{1,0:T(8,128)(2,1)S(1)} %get-tuple-element.4), kind=kLoop, calls=%fused_computation.25 | loop fusion | flops 786432 | bytes 2097152 | tf_op jit(solution)/shard_map/convert_element_type | solution.py:73
  (21 shorter events, 0.2 us)
Async XLA Ops:
  7.2 50.6 %copy-start = (bf16[256,1024]{1,0:T(8,128)(2,1)S(1)}, bf16[256,1024]{1,0:T(8,128)(2,1)}, u32[]{:S(2)}) copy-start(bf16[256,1024]{1,0:T(8,128)(2,1)} %param.24) | copy-start | bytes 1572868
  7.2 85.8 %all-reduce.3.cloned.1.call-start = ((), (), s32[]{:S(2)}) async-start(), calls=%async_computation | async-start | bytes 2097152 | tf_op jit(solution)/shard_map/psum | solution.py:69
  47.2 12.2 %copy-start.3 = (bf16[1024]{0:T(1024)(128)(2,1)S(1)}, bf16[1024]{0:T(1024)(128)(2,1)}, u32[]{:S(2)}) copy-start(bf16[1024]{0:T(1024)(128)(2,1)} %param.25) | copy-start | bytes 6148
  47.2 45.7 %copy-start.1 = (bf16[256,1024]{1,0:T(8,128)(2,1)S(1)}, bf16[256,1024]{1,0:T(8,128)(2,1)}, u32[]{:S(2)}) copy-start(bf16[256,1024]{1,0:T(8,128)(2,1)} %param.15) | copy-start | bytes 1572868
  47.2 47.2 %copy-start.4 = (bf16[1024,32]{0,1:T(8,128)(2,1)S(1)}, bf16[1024,32]{0,1:T(8,128)(2,1)}, u32[]{:S(2)}) copy-start(bf16[1024,32]{0,1:T(8,128)(2,1)} %param.26) | copy-start | bytes 196612
  47.3 47.5 %copy-start.2 = (s32[256,8]{0,1:T(8,128)S(1)}, s32[256,8]{0,1:T(8,128)}, u32[]{:S(2)}) copy-start(s32[256,8]{0,1:T(8,128)} %param.19) | copy-start | bytes 24580
  59.1 87.5 %all-reduce.5.cloned.1.call-start = ((), (), s32[]{:S(2)}) async-start(), calls=%async_computation.1 | async-start | bytes 2097152 | tf_op jit(solution)/shard_map/psum | solution.py:72
Sparse Core Ops, SparseCore 0:
  59.3 33.6 all-reduce.2
  115.5 31.0 all-reduce.4
where the time goes:
time: 156 us
  waiting for transfers between devices  64.8 us (42%)
  matrix products  44.8 us (29%)
  other arithmetic  30.2 us (19%)
  between operations  14.3 us (9%)
    psum x1, waiting for transfers between devices, layer_shard(): attn_sum = lax.psum(attn_local, 'tp')  33.5 us
    psum x1, waiting for transfers between devices, layer_shard(): moe_sum = lax.psum(moe_local, 'tp')  31.3 us
    select_n x1, other arithmetic, attention_part(): k_next = jnp.where(new_slot, k_new[:, None, :, :], k_cache)  22.2 us
    dot_general x1, matrix products, experts_part(): jnp.einsum('bef,efd->bd', inner_act, w_down, preferred_element_type=jnp.f...  12.7 us
    dot_general x1, matrix products, attention_part(): jnp.einsum('bkgs,bskd->bkgd', attn_weights, v_next, preferred_element_typ...  10.3 us
    dot_general x1, matrix products, experts_part(): jnp.einsum('bd,edf->bef', h_moe, w_gate, preferred_element_type=jnp.float32)  7.72 us
    sub x1, matrix products, attention_part(): jax.nn.softmax(jnp.where(in_range, scores, MASK_FILL), axis=-1)  7.69 us
  transfers between devices with their start and end apart: 2, of which 2 were waited for; matrix products, arithmetic and copies ran while one was open for 0% of the time, Pallas kernels for 0%

commit v1 on v0

v1 whole, which is shorter than its diff:
```python
import jax
import jax.numpy as jnp
import numpy as np
from jax import lax
from jax.experimental import pallas as pl
from jax.experimental.pallas import tpu as pltpu
from jax.sharding import PartitionSpec as P

EPSILON = 1e-5
ROPE_THETA = 1000000.0
MASK_FILL = -1e30
BLOCK = 16
SLOTS = 8
AHEAD = 4
GROUP = 4


def normed(vector32, gain32):
    scale = lax.rsqrt(jnp.mean(vector32 * vector32, axis=-1, keepdims=True) + EPSILON)
    return (vector32 * scale * gain32).astype(jnp.bfloat16)


def attention_kernel(seq_s, seq_v, freq, gain, hidden, w_q, w_k, w_v, k_in, v_in, o_out, k_out, v_out,
                     hid, wqkv, kv_col, q_rows, o_rows, kbuf, vbuf, w_sem, k_rd, v_rd, k_wr, v_wr):
    rows, width, slots = k_in.shape
    heads_w = w_q.shape[1]
    half = width // 4
    steps = rows // BLOCK

    def read(i, slot):
        src = pl.ds(i * BLOCK, BLOCK)
        return (pltpu.make_async_copy(k_in.at[src], kbuf.at[slot], k_rd.at[slot]),
                pltpu.make_async_copy(v_in.at[src], vbuf.at[slot], v_rd.at[slot]))

    def write(i, slot):
        dst = pl.ds(i * BLOCK, BLOCK)
        return (pltpu.make_async_copy(kbuf.at[slot], k_out.at[dst], k_wr.at[slot]),
                pltpu.make_async_copy(vbuf.at[slot], v_out.at[dst], v_wr.at[slot]))

    loads = [pltpu.make_async_copy(hidden, hid, w_sem.at[0]),
             pltpu.make_async_copy(w_q, wqkv.at[:, 0:heads_w], w_sem.at[1]),
             pltpu.make_async_copy(w_k, wqkv.at[:, heads_w:heads_w + width], w_sem.at[2]),
             pltpu.make_async_copy(w_v, wqkv.at[:, heads_w + width:], w_sem.at[3])]
    for copy in loads:
        copy.start()
    for i in range(SLOTS):
        for copy in read(i, i):
            copy.start()
    angles = freq[...] * seq_v[...].astype(jnp.float32)
    cos_t, sin_t = jnp.cos(angles), jnp.sin(angles)
    for copy in loads:
        copy.wait()
    h = normed(hid[...].astype(jnp.float32), gain[...].astype(jnp.float32))
    qkv_t = jnp.dot(h, wqkv[...], preferred_element_type=jnp.float32).T

    def rotated(at):
        a, c = qkv_t[at:at + half], qkv_t[at + half:at + 2 * half]
        return [a * cos_t - c * sin_t, c * cos_t + a * sin_t]

    k_t = jnp.concatenate(rotated(heads_w) + rotated(heads_w + 2 * half), axis=0)
    v_t = qkv_t[heads_w + width:]
    for part in range(rows // 128):
        lanes = slice(part * 128, part * 128 + 128)
        kv_col[part, 0:width] = k_t[:, lanes].astype(jnp.bfloat16)
        kv_col[part, width:] = v_t[:, lanes].astype(jnp.bfloat16)
    lane = lax.broadcasted_iota(jnp.int32, (rows, width), 1)
    for g in range(2):
        q_g = jnp.concatenate(rotated(g * 2 * half) + rotated((2 + g) * 2 * half), axis=0).T
        q_g = q_g.astype(jnp.bfloat16).astype(jnp.float32) * 0.125
        for kv in range(2):
            keep = (lane < 2 * half) if kv == 0 else (lane >= 2 * half)
            q_rows[pl.ds(kv * 2 + g, rows, stride=8), :] = jnp.where(keep, q_g, 0.0)
    for r in range(4, 8):
        q_rows[pl.ds(r, rows, stride=8), :] = jnp.zeros((rows, width), jnp.float32)

    slot_id = lax.broadcasted_iota(jnp.int32, (8, slots), 1)
    slot_bf = lax.broadcasted_iota(jnp.int32, (width, slots), 1).astype(jnp.float32).astype(jnp.bfloat16)

    row_id = lax.broadcasted_iota(jnp.int32, (128, 256), 0) - lax.div(lax.broadcasted_iota(jnp.int32, (128, 256), 1), 128)
    row_bf = row_id.astype(jnp.float32).astype(jnp.bfloat16)

    def step(i, carry):
        slot = lax.rem(i, SLOTS)
        for copy in read(i, slot):
            copy.wait()
        per = 128 // BLOCK
        columns = kv_col[lax.div(i, per)]
        first_row = lax.rem(i, per) * BLOCK
        cols = []
        for j in range(0, BLOCK, 2):
            pick = (row_bf == (first_row + j).astype(jnp.float32).astype(jnp.bfloat16))
            pick = jnp.where(pick, jnp.ones((), jnp.bfloat16), jnp.zeros((), jnp.bfloat16))
            both = jnp.dot(columns, pick, preferred_element_type=jnp.float32).astype(jnp.bfloat16)
            cols += [both[:, 0:128], both[:, 128:256]]
        places = [seq_s[i * BLOCK + j] for j in range(BLOCK)]

        def updated(buf, j, at):
            col = jnp.concatenate([cols[j][at:at + width]] * (slots // 128), axis=1)
            here = slot_bf == places[j].astype(jnp.float32).astype(jnp.bfloat16)
            new = jnp.where(here, col, buf[slot, j])
            buf[slot, j] = new
            return new

        scores = []
        for j in range(BLOCK):
            q = q_rows[pl.ds((i * BLOCK + j) * 8, 8), :].astype(jnp.bfloat16)
            s = jnp.dot(q, updated(kbuf, j, 0), preferred_element_type=jnp.float32)
            scores.append(jnp.where(slot_id <= places[j], s, MASK_FILL))
        for j in range(BLOCK):
            s = scores[j]
            e = jnp.exp(s - jnp.max(s, axis=-1, keepdims=True))
            w = (e / jnp.sum(e, axis=-1, keepdims=True)).astype(jnp.bfloat16)
            o = lax.dot_general(w, updated(vbuf, j, width), (((1,), (1,)), ((), ())), preferred_element_type=jnp.float32)
            o_rows[pl.ds(j * 8, 8), :] = o
        for copy in write(i, slot):
            copy.start()
        low = lax.broadcasted_iota(jnp.int32, (BLOCK, width), 1) < 2 * half
        for kv in range(2):
            first = o_rows[pl.ds(2 * kv, BLOCK, stride=8), :]
            second = o_rows[pl.ds(2 * kv + 1, BLOCK, stride=8), :]
            if kv == 0:
                second = pltpu.roll(second, 2 * half, axis=1)
            else:
                first = pltpu.roll(first, 2 * half, axis=1)
            o_out[pl.ds(i * BLOCK, BLOCK), kv * width:(kv + 1) * width] = jnp.where(low, first, second).astype(jnp.bfloat16)

        @pl.when(jnp.logical_and(i >= AHEAD, i < steps - SLOTS + AHEAD))
        def _():
            old = lax.rem(i + SLOTS - AHEAD, SLOTS)
            for copy in write(i - AHEAD, old):
                copy.wait()
            for copy in read(i + SLOTS - AHEAD, old):
                copy.start()
        return carry

    lax.fori_loop(0, steps, step, 0)
    for i in range(steps - SLOTS, steps):
        for copy in write(i, i % SLOTS):
            copy.wait()


def attention_call(hidden_in, k_t, v_t, seq_lens, g_attn, w_q, w_k, w_v):
    rows, width, slots = k_t.shape
    any_spec = pl.BlockSpec(memory_space=pltpu.HBM)
    vmem = pl.BlockSpec(memory_space=pltpu.VMEM)
    freq = (ROPE_THETA ** (-np.arange(0, 64, 2) / 64)).astype(np.float32)
    cache = jax.ShapeDtypeStruct(k_t.shape, k_t.dtype)
    dma = pltpu.SemaphoreType.DMA
    return pl.pallas_call(
        attention_kernel,
        out_shape=(jax.ShapeDtypeStruct((rows, w_q.shape[1]), jnp.bfloat16), cache, cache),
        in_specs=[pl.BlockSpec(memory_space=pltpu.SMEM), vmem, vmem, vmem] + [any_spec] * 6,
        out_specs=(vmem, any_spec, any_spec),
        scratch_shapes=[
            pltpu.VMEM(hidden_in.shape, jnp.bfloat16),
            pltpu.VMEM((hidden_in.shape[1], w_q.shape[1] + 2 * width), jnp.bfloat16),
            pltpu.VMEM((rows // 128, 2 * width, 128), jnp.bfloat16),
            pltpu.VMEM((rows * 8, width), jnp.float32),
            pltpu.VMEM((BLOCK * 8, width), jnp.float32),
            pltpu.VMEM((SLOTS, BLOCK, width, slots), jnp.bfloat16),
            pltpu.VMEM((SLOTS, BLOCK, width, slots), jnp.bfloat16),
            dma((4,)), dma((SLOTS,)), dma((SLOTS,)), dma((SLOTS,)), dma((SLOTS,)),
        ],
        compiler_params=pltpu.CompilerParams(vmem_limit_bytes=60 << 20),
        cost_estimate=pl.CostEstimate(flops=10**9, bytes_accessed=70 * 10**6, transcendentals=0),
        name="attention",
    )(seq_lens, seq_lens.reshape(1, rows), freq.reshape(32, 1), g_attn.reshape(1, -1), hidden_in, w_q, w_k, w_v, k_t, v_t)


def expert_kernel(o_in, chosen, gain, router, hidden, wo_own, wo_peer, w_gate, w_up, w_down, out,
                  hid, wo_full, o_full, w_in, w_dn, x1, h2_buf, gates, z, acc, from_pair, chip_sum, from_far,
                  ld_sem, wi_sem, wd_sem, wo_snd, wo_rcv, o_snd, o_rcv, a_snd, a_rcv, b_snd, b_rcv, c_snd, c_rcv):
    experts, dim, part = w_gate.shape
    rows = hid.shape[0]
    half = rows // 2
    quarter, eighth = half // 2, half // 4
    cols = dim // 2
    groups = w_in.shape[0] // GROUP
    me = lax.axis_index("tp")
    core, chip = lax.rem(me, 2), lax.div(me, 2)
    pair, far = me + 1 - 2 * core, me + 2 - 4 * chip
    pair_far = far + 1 - 2 * core

    def remote(src, dst, send, recv, to):
        return pltpu.make_async_remote_copy(src_ref=src, dst_ref=dst, send_sem=send, recv_sem=recv,
                                            device_id={"tp": to}, device_id_type=pl.DeviceIdType.MESH)

    def load_in(g):
        sl = pl.ds(g * GROUP, GROUP)
        return (pltpu.make_async_copy(w_gate.at[sl], w_in.at[sl, :, 0:part], wi_sem.at[0, g]),
                pltpu.make_async_copy(w_up.at[sl], w_in.at[sl, :, part:2 * part], wi_sem.at[1, g]))

    def load_down(g):
        sl = pl.ds(g * (w_dn.shape[0] // 4), w_dn.shape[0] // 4)
        return pltpu.make_async_copy(w_down.at[sl], w_dn.at[sl], wd_sem.at[g])

    loads = [pltpu.make_async_copy(hidden, hid, ld_sem.at[0]),
             pltpu.make_async_copy(wo_own, wo_full.at[me], ld_sem.at[1]),
             pltpu.make_async_copy(wo_peer, wo_full.at[far], ld_sem.at[2])]
    for copy in loads:
        copy.start()
    for g in range(groups):
        for copy in load_in(g):
            copy.start()
    for g in range(4):
        load_down(g).start()

    barrier = pltpu.get_barrier_semaphore()
    for peer in (pair, far):
        pl.semaphore_signal(barrier, inc=1, device_id={"tp": peer}, device_id_type=pl.DeviceIdType.MESH)
    pl.semaphore_wait(barrier, 2)

    def o_block(owner, h, kind, to):
        src = o_in.at[pl.ds(h * half, half)] if kind < 2 else o_full.at[owner, pl.ds(h * half, half)]
        return remote(src, o_full.at[owner, pl.ds(h * half, half)], o_snd.at[kind, h], o_rcv.at[kind, h], to)

    sends = []

    def go(copy):
        copy.start()
        sends.append(copy)

    for h in range(2):
        go(o_block(me, h, 0, far))
    for h in range(2):
        go(o_block(me, h, 1, pair))
    go(remote(wo_own, wo_full.at[me], wo_snd.at[0], wo_rcv.at[0], pair))
    go(remote(wo_peer, wo_full.at[far], wo_snd.at[1], wo_rcv.at[1], pair))
    o_full[me] = o_in[...]

    def relay_o(h):
        o_block(far, h, 0, far).wait_recv()
        go(o_block(far, h, 2, pair))

    def mid(h):
        o_block(pair, h, 1, pair).wait_recv()
        o_block(pair_far, h, 2, pair).wait_recv()
        at = pl.ds(h * half, half)
        total = hid[at, :].astype(jnp.float32)
        for r in range(4):
            total = total + jnp.dot(o_full[r, at, :], wo_full[r], preferred_element_type=jnp.float32)
        x1[at, :] = total.astype(jnp.bfloat16)

    def routed(h):
        at = pl.ds(h * half, half)
        h2 = normed(x1[at, :].astype(jnp.float32), gain[...].astype(jnp.float32))
        logits = lax.dot_general(router[...], h2, (((1,), (1,)), ((), ())), preferred_element_type=jnp.float32)
        expert_id = lax.broadcasted_iota(jnp.int32, logits.shape, 0)
        picks = chosen[:, h * half:(h + 1) * half]
        hit = expert_id == picks[0:1]
        for k in range(1, picks.shape[0]):
            hit = jnp.logical_or(hit, expert_id == picks[k:k + 1])
        shown = jnp.where(hit, logits, MASK_FILL)
        e = jnp.where(hit, jnp.exp(shown - jnp.max(shown, axis=0, keepdims=True)), 0.0)
        g = e / jnp.sum(e, axis=0, keepdims=True)
        gates[h] = jnp.concatenate([g, jnp.zeros((128 - experts, half), jnp.float32)], axis=0).T
        return h2

    lane = lax.broadcasted_iota(jnp.int32, (half, 128), 1)

    def inner(h, h2_ref, lo, hi):
        def group(g, carry):
            if h == 0:
                for copy in load_in(g):
                    copy.wait()
            for k in range(GROUP):
                e = g * GROUP + k
                both = jnp.dot(h2_ref[...], w_in[e], preferred_element_type=jnp.float32)
                gate, up = both[:, :part], both[:, part:]
                weight = jnp.sum(jnp.where(lane == e, gates[h], 0.0), axis=1, keepdims=True)
                act = weight * (gate / (1.0 + jnp.exp(-gate))) * up
                z[:, pl.ds(pl.multiple_of(e * part, part), part)] = act.astype(jnp.bfloat16)
            return carry
        lax.fori_loop(lo, hi, group, 0)

    def down(h, c):
        acc[h, c] = jnp.dot(z[...], w_dn[:, c * cols:(c + 1) * cols], preferred_element_type=jnp.float32)

    def pair_copy(h, c):
        return remote(acc.at[h, c, pl.ds((1 - core) * quarter, quarter)], from_pair.at[h, c], a_snd.at[h, c], a_rcv.at[h, c], pair)

    def far_copy(h, c):
        return remote(chip_sum.at[h, c, pl.ds((1 - chip) * eighth, eighth)], from_far.at[h, c], b_snd.at[h, c], b_rcv.at[h, c], far)

    def out_copy(h, c, kind, block_core, block_chip, to):
        at = out.at[pl.ds(h * half + block_core * quarter + block_chip * eighth, eighth), c * cols:(c + 1) * cols]
        return remote(at, at, c_snd.at[kind, h, c], c_rcv.at[kind, h, c], to)

    def stage_b(h, c):
        pair_copy(h, c).wait_recv()
        chip_sum[h, c] = acc[h, c, pl.ds(core * quarter, quarter)] + from_pair[h, c]
        go(far_copy(h, c))

    def stage_c(h, c):
        far_copy(h, c).wait_recv()
        at = pl.ds(h * half + core * quarter + chip * eighth, eighth)
        cut = slice(c * cols, (c + 1) * cols)
        total = chip_sum[h, c, pl.ds(chip * eighth, eighth)] + from_far[h, c]
        out[at, cut] = (x1[at, cut].astype(jnp.float32) + total).astype(jnp.bfloat16)
        go(out_copy(h, c, 0, core, chip, far))
        go(out_copy(h, c, 1, core, chip, pair))

    def stage_d(h, c):
        out_copy(h, c, 0, core, 1 - chip, far).wait_recv()
        go(out_copy(h, c, 2, core, 1 - chip, pair))

    def stage_e(h, c):
        out_copy(h, c, 1, 1 - core, chip, pair).wait_recv()
        out_copy(h, c, 2, 1 - core, 1 - chip, pair).wait_recv()

    relay_o(0)
    for copy in loads:
        copy.wait()
    remote(wo_own, wo_full.at[pair], wo_snd.at[0], wo_rcv.at[0], pair).wait_recv()
    remote(wo_peer, wo_full.at[pair_far], wo_snd.at[1], wo_rcv.at[1], pair).wait_recv()
    mid(0)
    relay_o(1)

    def with_h2(h, h2_ref):
        h2_ref[...] = routed(h)

    def first_half(h2_ref):
        with_h2(0, h2_ref)
        inner(0, h2_ref, 0, groups)
        for g in range(4):
            load_down(g).wait()
        for c in range(2):
            down(0, c)
            go(pair_copy(0, c))
        mid(1)
        with_h2(1, h2_ref)
        for c in range(2):
            stage_b(0, c)
        inner(1, h2_ref, 0, groups // 2)
        for c in range(2):
            stage_c(0, c)
        inner(1, h2_ref, groups // 2, groups)
        for c in range(2):
            stage_d(0, c)
        for c in range(2):
            down(1, c)
            go(pair_copy(1, c))

    first_half(h2_buf)
    for stage in (stage_b, stage_c, stage_d):
        for c in range(2):
            stage(1, c)
    for h in range(2):
        for c in range(2):
            stage_e(h, c)
    for copy in sends:
        copy.wait_send()


def expert_call(o, hidden_in, chosen_t, g_moe, router_t, w_o, wo_peer, w_gate, w_up, w_down):
    rows, dim = hidden_in.shape
    experts, _, part = w_gate.shape
    half, cols = rows // 2, dim // 2
    any_spec = pl.BlockSpec(memory_space=pltpu.HBM)
    vmem = pl.BlockSpec(memory_space=pltpu.VMEM)
    dma = pltpu.SemaphoreType.DMA
    bf, f32 = jnp.bfloat16, jnp.float32
    return pl.pallas_call(
        expert_kernel,
        out_shape=jax.ShapeDtypeStruct((rows, dim), bf),
        in_specs=[vmem] * 4 + [any_spec] * 6,
        out_specs=vmem,
        scratch_shapes=[
            pltpu.VMEM((rows, dim), bf),
            pltpu.VMEM((4,) + w_o.shape, bf),
            pltpu.VMEM((4,) + o.shape, bf),
            pltpu.VMEM((experts, dim, 2 * part), bf),
            pltpu.VMEM((experts * part, dim), bf),
            pltpu.VMEM((rows, dim), bf),
            pltpu.VMEM((half, dim), bf),
            pltpu.VMEM((2, half, 128), f32),
            pltpu.VMEM((half, experts * part), bf),
            pltpu.VMEM((2, 2, half, cols), f32),
            pltpu.VMEM((2, 2, half // 2, cols), f32),
            pltpu.VMEM((2, 2, half // 2, cols), f32),
            pltpu.VMEM((2, 2, half // 4, cols), f32),
            dma((3,)), dma((2, experts // GROUP)), dma((4,)), dma((2,)), dma((2,)), dma((3, 2)), dma((3, 2)),
            dma((2, 2)), dma((2, 2)), dma((2, 2)), dma((2, 2)), dma((3, 2, 2)), dma((3, 2, 2)),
        ],
        compiler_params=pltpu.CompilerParams(collective_id=0, has_side_effects=True, vmem_limit_bytes=60 << 20),
        cost_estimate=pl.CostEstimate(flops=7 * 10**9, bytes_accessed=28 * 10**6, transcendentals=0),
        name="experts",
    )(o, chosen_t, g_moe.reshape(1, -1), router_t, hidden_in, w_o, wo_peer, w_gate, w_up, w_down.reshape(experts * part, dim))


def solution(mesh):
    cache_spec = P("dp", None, "tp", None)
    in_specs = (P("dp", None), cache_spec, cache_spec, P("dp"), P("dp", None), P(None), P(None, "tp"), P(None, "tp"), P(None, "tp"), P("tp", None), P(None), P(None, None), P(None, None, "tp"), P(None, None, "tp"), P(None, "tp", None))
    out_specs = (P("dp", None), cache_spec, cache_spec)

    def layer_shard(hidden_in, k_cache, v_cache, seq_lens, chosen_experts, g_attn, w_q, w_k, w_v, w_o, g_moe, w_router, w_gate, w_up, w_down):
        rows, slots, kvh, hd = k_cache.shape
        as_t = lambda c: c.transpose(0, 2, 3, 1).reshape(rows, kvh * hd, slots)
        back = lambda c: c.reshape(rows, kvh, hd, slots).transpose(0, 3, 1, 2)
        wo_peer = lax.ppermute(w_o, "tp", [(0, 2), (1, 3), (2, 0), (3, 1)])
        o, k_n, v_n = attention_call(hidden_in, as_t(k_cache), as_t(v_cache), seq_lens, g_attn, w_q, w_k, w_v)
        hidden_out = expert_call(o, hidden_in, chosen_experts.T, g_moe, w_router.T, w_o, wo_peer, w_gate, w_up, w_down)
        return hidden_out, back(k_n), back(v_n)

    return jax.shard_map(layer_shard, mesh=mesh, in_specs=in_specs, out_specs=out_specs, check_vma=False)
```

time: 156 us -> 73.4 us (0.47)
  waiting for transfers between devices: 64.8 us -> 0.01 us
  Pallas kernels: 0 us -> 63.9 us
  matrix products: 44.8 us -> 0 us
  other arithmetic: 30.2 us -> 0 us
  between operations: 14.3 us -> 0.66 us
  local copies, waits for them, and re-layouts: 1.28 us -> 5.21 us
  starting transfers between devices: 0.26 us -> 3.36 us
    psum x2 -> x0, waiting for transfers between devices: 64.8 us -> none  [the longest x1 33.5 us: layer_shard(): attn_sum = lax.psum(attn_local, 'tp')]
    pallas_call x0 -> x2, Pallas kernels: none -> 63.9 us  [the longest x1 35.4 us: expert_call(): pl.pallas_call(expert_kernel, out_shape=jax.ShapeDtypeStruct((rows, dim),...]
    dot_general x8 -> x0, matrix products: 37.1 us -> none  [the longest x1 12.7 us: experts_part(): jnp.einsum('bef,efd->bd', inner_act, w_down, preferred_element_type=jnp.f...]
    select_n x1 -> x0, other arithmetic: 22.2 us -> none  [attention_part(): k_next = jnp.where(new_slot, k_new[:, None, :, :], k_cache)]
    sub x1 -> x0, matrix products: 7.69 us -> none  [attention_part(): jax.nn.softmax(jnp.where(in_range, scores, MASK_FILL), axis=-1)]
    convert_element_type x4 -> x0, other arithmetic: 3.59 us -> none  [the longest x1 2.16 us: layer_shard(): hidden_out = (hidden_mid.astype(jnp.float32) + moe_sum).astype(jnp.bfloat16)]
    ppermute x0 -> x1, starting transfers between devices: none -> 3.36 us  [layer_shard(): wo_peer = lax.ppermute(w_o, 'tp', [(0, 2), (1, 3), (2, 0), (3, 1)])]
    reduce_sum x5 -> x0, other arithmetic: 2.78 us -> none  [the longest x2 2.68 us: rms_norm(): jnp.mean(vector32 * vector32, axis=-1, keepdims=True) + EPSILON]
  transfers between devices with their start and end apart: 2 -> 1, of which waited for: 2 -> 0; matrix products, arithmetic and copies ran while one was open for 0% -> 3% of each run, Pallas kernels for 0% -> 39%
where the time goes in v1:
time: 73.4 us; the launch traced here: 73.1 us
  Pallas kernels  63.9 us (87%)
  local copies, waits for them, and re-layouts  5.21 us (7%)
  starting transfers between devices  3.36 us (5%)
    pallas_call x1, Pallas kernels, expert_call(): pl.pallas_call(expert_kernel, out_shape=jax.ShapeDtypeStruct((rows, dim),...  35.4 us
    pallas_call x1, Pallas kernels, attention_call(): pl.pallas_call(attention_kernel, out_shape=(jax.ShapeDtypeStruct((rows, w...  28.5 us
    ppermute x1, starting transfers between devices, layer_shard(): wo_peer = lax.ppermute(w_o, 'tp', [(0, 2), (1, 3), (2, 0), (3, 1)])  3.36 us
    unnamed x3, local copies, waits for them, and re-layouts  2.66 us
  transfers between devices with their start and end apart: 1, of which 0 were waited for; matrix products, arithmetic and copies ran while one was open for 3% of the time, Pallas kernels for 39%

profile of v1, /device:TPU:0, one launch (start us, length us, event | category | flops | bytes accessed | tf_op | source)
XLA Modules:
  0.0 73.1 jit_solution(3259221749440484812)
XLA Ops:
  0.6 3.4 %collective-permute-start = (bf16[256,1024]{1,0:T(8,128)(2,1)}, bf16[256,1024]{1,0:T(8,128)(2,1)S(1)}, u32[]{:S(2)}, u32[]{:S(2)}) collective-permute-start(bf16[256,1024]{1,0:T(8,128)(2,1)} %wo_own.1), channel_id=1, source_target_pairs={{0,2},{1,3},{2,0},{3,1},{4,6},{5,7},{6,4},{7,5}} | collective-permute-start | bytes 1572872 | tf_op jit(solution)/shard_map/ppermute | solution.py:400
  4.0 1.3 %reshape.31.gain = bf16[1,1024]{1,0:T(2,128)(2,1)} reshape(bf16[1024]{0:T(1024)(128)(2,1)} %param.21) | data formatting | bytes 4096 | tf_op jit(solution)/shard_map/reshape | solution.py:167
  5.3 1.3 %reshape.34.gain = bf16[1,1024]{1,0:T(2,128)(2,1)} reshape(bf16[1024]{0:T(1024)(128)(2,1)} %param.26) | data formatting | bytes 4096 | tf_op jit(solution)/shard_map/reshape | solution.py:388
  6.5 28.5 %attention.1 = (bf16[256,256]{1,0:T(8,128)(2,1)}, bf16[256,128,256]{2,1,0:T(8,128)(2,1)}, bf16[256,128,256]{2,1,0:T(8,128)(2,1)}) custom-call(s32[256]{0:T(256)} %seq_s.1, s32[1,256]{1,0:T(1,128)} %bitcast.21, f32[32,1]{1,0:T(8,128)} %constant.2.clone.freq, bf16[1,1024]{1,0:T(2,128)(2,1)} %reshape.31.gain, bf16[256,1024]{1,0:T(8,128)(2,1)} %hidden.3, ...), custom_call_target="tpu_custom_call" | custom-call | flops 1000000000 | bytes 70000000 | tf_op jit(solution)/shard_map/attention/pallas_call | solution.py:149
  35.0 0.0 collective-permute-done.wo_peer
  35.0 0.0 copy-start
  35.0 0.8 %copy-done = bf16[256,1024]{1,0:T(8,128)(2,1)} copy-done((bf16[256,1024]{1,0:T(8,128)(2,1)}, bf16[256,1024]{1,0:T(8,128)(2,1)S(1)}, u32[]{:S(2)}) %copy-start) | copy-done | bytes 524312
  35.8 35.4 %experts.1 = bf16[256,1024]{1,0:T(8,128)(2,1)} custom-call(bf16[256,256]{1,0:T(8,128)(2,1)} %get-tuple-element.6.o_in, s32[8,256]{1,0:T(8,128)} %bitcast.20, bf16[1,1024]{1,0:T(2,128)(2,1)} %reshape.34.gain, bf16[32,1024]{1,0:T(8,128)(2,1)} %bitcast.19, bf16[256,1024]{1,0:T(8,128)(2,1)} %hidden.3, bf16[256,1024]{1,0:T(8,128)(2,1)} %wo_own.1, ...), custom_call_target="tpu_custom_call" | custom-call | flops 7000000000 | bytes 28000000 | tf_op jit(solution)/shard_map/experts/pallas_call | solution.py:363
  71.3 1.9 %copy.20 = bf16[256,1024]{1,0:T(8,128)(2,1)} copy(bf16[256,1024]{1,0:T(8,128)(2,1)} %experts.1) | data formatting | bytes 1048576
Async XLA Ops:
  0.6 34.4 %collective-permute-start = (bf16[256,1024]{1,0:T(8,128)(2,1)}, bf16[256,1024]{1,0:T(8,128)(2,1)S(1)}, u32[]{:S(2)}, u32[]{:S(2)}) collective-permute-start(bf16[256,1024]{1,0:T(8,128)(2,1)} %wo_own.1), channel_id=1, source_target_pairs={{0,2},{1,3},{2,0},{3,1},{4,6},{5,7},{6,4},{7,5}} | collective-permute-start | bytes 1572872 | tf_op jit(solution)/shard_map/ppermute | solution.py:400
  35.0 0.8 %copy-start = (bf16[256,1024]{1,0:T(8,128)(2,1)}, bf16[256,1024]{1,0:T(8,128)(2,1)S(1)}, u32[]{:S(2)}) copy-start(bf16[256,1024]{1,0:T(8,128)(2,1)S(1)} %collective-permute-done.wo_peer) | copy-start | bytes 1572868

commit v2 on v1

v2 whole, which is shorter than its diff:
```python
import math
import jax
import jax.numpy as jnp
from jax import lax
from jax.experimental import pallas as pl
from jax.experimental.pallas import tpu as pltpu
from jax.sharding import PartitionSpec as P

EPSILON = 1e-5
ROPE_THETA = 1000000.0
MASK_FILL = -1e30
BLOCK = 16
SLOTS = 8
AHEAD = 4
GROUP = 4
UNROLL = 8
PARTS = 2
CHUNKS = 2
DIRECT = 0


def pinned(array):
    return pltpu.with_memory_space_constraint(array, pltpu.HBM)


def normed(vector32, gain32):
    scale = lax.rsqrt(jnp.mean(vector32 * vector32, axis=-1, keepdims=True) + EPSILON)
    return (vector32 * scale * gain32).astype(jnp.bfloat16)


def attention_kernel(seq_lens, g_attn, hidden, w_q, w_k, w_v, k_in, v_in, o_out, k_out, v_out,
                     seq_s, seq_v, gain, hid, wqkv, kv_col, q_rows, o_rows, kbuf, vbuf, w_sem, k_rd, v_rd, k_wr, v_wr):
    rows, width, slots = k_in.shape
    heads_w = w_q.shape[1]
    half = width // 4
    steps = rows // BLOCK

    def read(i, slot):
        src = pl.ds(i * BLOCK, BLOCK)
        return (pltpu.make_async_copy(k_in.at[src], kbuf.at[slot], k_rd.at[slot]),
                pltpu.make_async_copy(v_in.at[src], vbuf.at[slot], v_rd.at[slot]))

    def write(i, slot):
        dst = pl.ds(i * BLOCK, BLOCK)
        return (pltpu.make_async_copy(kbuf.at[slot], k_out.at[dst], k_wr.at[slot]),
                pltpu.make_async_copy(vbuf.at[slot], v_out.at[dst], v_wr.at[slot]))

    loads = [pltpu.make_async_copy(hidden, hid, w_sem.at[0]),
             pltpu.make_async_copy(w_q, wqkv.at[:, 0:heads_w], w_sem.at[1]),
             pltpu.make_async_copy(w_k, wqkv.at[:, heads_w:heads_w + width], w_sem.at[2]),
             pltpu.make_async_copy(w_v, wqkv.at[:, heads_w + width:], w_sem.at[3]),
             pltpu.make_async_copy(seq_lens, seq_v, w_sem.at[4]),
             pltpu.make_async_copy(seq_lens, seq_s, w_sem.at[5]),
             pltpu.make_async_copy(g_attn, gain, w_sem.at[6])]
    for copy in loads:
        copy.start()
    for i in range(SLOTS):
        for copy in read(i, i):
            copy.start()
    loads[4].wait()
    place = lax.broadcasted_iota(jnp.int32, (half, rows), 0).astype(jnp.float32)
    angles = jnp.exp(place * (-math.log(ROPE_THETA) / half)) * seq_v[...].astype(jnp.float32)[None, :]
    cos_t, sin_t = jnp.cos(angles), jnp.sin(angles)
    for copy in loads[:4] + loads[5:]:
        copy.wait()
    h = normed(hid[...].astype(jnp.float32), gain[...].astype(jnp.float32))
    qkv_t = jnp.dot(h, wqkv[...], preferred_element_type=jnp.float32).T

    def rotated(at):
        a, c = qkv_t[at:at + half], qkv_t[at + half:at + 2 * half]
        return [a * cos_t - c * sin_t, c * cos_t + a * sin_t]

    k_t = jnp.concatenate(rotated(heads_w) + rotated(heads_w + 2 * half), axis=0)
    v_t = qkv_t[heads_w + width:]
    for part in range(rows // 128):
        lanes = slice(part * 128, part * 128 + 128)
        kv_col[part, 0:width] = k_t[:, lanes].astype(jnp.bfloat16)
        kv_col[part, width:] = v_t[:, lanes].astype(jnp.bfloat16)
    lane = lax.broadcasted_iota(jnp.int32, (rows, width), 1)
    for g in range(2):
        q_g = jnp.concatenate(rotated(g * 2 * half) + rotated((2 + g) * 2 * half), axis=0).T
        q_g = q_g.astype(jnp.bfloat16).astype(jnp.float32) * 0.125
        for kv in range(2):
            keep = (lane < 2 * half) if kv == 0 else (lane >= 2 * half)
            q_rows[pl.ds(kv * 2 + g, rows, stride=8), :] = jnp.where(keep, q_g, 0.0)
    for r in range(4, 8):
        q_rows[pl.ds(r, rows, stride=8), :] = jnp.zeros((rows, width), jnp.float32)

    slot_id = lax.broadcasted_iota(jnp.int32, (8, slots), 1)
    slot_bf = lax.broadcasted_iota(jnp.int32, (width, slots), 1).astype(jnp.float32).astype(jnp.bfloat16)

    row_id = lax.broadcasted_iota(jnp.int32, (128, 256), 0) - lax.div(lax.broadcasted_iota(jnp.int32, (128, 256), 1), 128)
    row_bf = row_id.astype(jnp.float32).astype(jnp.bfloat16)

    def step(i, carry):
        slot = lax.rem(i, SLOTS)
        for copy in read(i, slot):
            copy.wait()
        per = 128 // BLOCK
        columns = kv_col[lax.div(i, per)]
        first_row = lax.rem(i, per) * BLOCK
        cols = []
        for j in range(0, BLOCK, 2):
            pick = (row_bf == (first_row + j).astype(jnp.float32).astype(jnp.bfloat16))
            pick = jnp.where(pick, jnp.ones((), jnp.bfloat16), jnp.zeros((), jnp.bfloat16))
            both = jnp.dot(columns, pick, preferred_element_type=jnp.float32).astype(jnp.bfloat16)
            cols += [both[:, 0:128], both[:, 128:256]]
        places = [seq_s[i * BLOCK + j] for j in range(BLOCK)]

        def updated(buf, j, at):
            col = jnp.concatenate([cols[j][at:at + width]] * (slots // 128), axis=1)
            here = slot_bf == places[j].astype(jnp.float32).astype(jnp.bfloat16)
            new = jnp.where(here, col, buf[slot, j])
            buf[slot, j] = new
            return new

        scores = []
        for j in range(BLOCK):
            q = q_rows[pl.ds((i * BLOCK + j) * 8, 8), :].astype(jnp.bfloat16)
            s = jnp.dot(q, updated(kbuf, j, 0), preferred_element_type=jnp.float32)
            scores.append(jnp.where(slot_id <= places[j], s, MASK_FILL))
        for j in range(BLOCK):
            s = scores[j]
            e = jnp.exp(s - jnp.max(s, axis=-1, keepdims=True))
            w = (e / jnp.sum(e, axis=-1, keepdims=True)).astype(jnp.bfloat16)
            o = lax.dot_general(w, updated(vbuf, j, width), (((1,), (1,)), ((), ())), preferred_element_type=jnp.float32)
            o_rows[pl.ds(j * 8, 8), :] = o
        for copy in write(i, slot):
            copy.start()
        low = lax.broadcasted_iota(jnp.int32, (BLOCK, width), 1) < 2 * half
        for kv in range(2):
            first = o_rows[pl.ds(2 * kv, BLOCK, stride=8), :]
            second = o_rows[pl.ds(2 * kv + 1, BLOCK, stride=8), :]
            if kv == 0:
                second = pltpu.roll(second, 2 * half, axis=1)
            else:
                first = pltpu.roll(first, 2 * half, axis=1)
            o_out[pl.ds(i * BLOCK, BLOCK), kv * width:(kv + 1) * width] = jnp.where(low, first, second).astype(jnp.bfloat16)

        @pl.when(jnp.logical_and(i >= AHEAD, i < steps - SLOTS + AHEAD))
        def _():
            old = lax.rem(i + SLOTS - AHEAD, SLOTS)
            for copy in write(i - AHEAD, old):
                copy.wait()
            for copy in read(i + SLOTS - AHEAD, old):
                copy.start()
        return carry

    lax.fori_loop(0, steps, step, 0)
    for i in range(steps - SLOTS, steps):
        for copy in write(i, i % SLOTS):
            copy.wait()


def attention_call(hidden_in, k_t, v_t, seq_lens, g_attn, w_q, w_k, w_v):
    rows, width, slots = k_t.shape
    any_spec = pl.BlockSpec(memory_space=pltpu.HBM)
    vmem = pl.BlockSpec(memory_space=pltpu.VMEM)
    cache = jax.ShapeDtypeStruct(k_t.shape, k_t.dtype)
    dma = pltpu.SemaphoreType.DMA
    return pl.pallas_call(
        attention_kernel,
        out_shape=(jax.ShapeDtypeStruct((rows, w_q.shape[1]), jnp.bfloat16), cache, cache),
        in_specs=[any_spec] * 8,
        out_specs=(vmem, any_spec, any_spec),
        scratch_shapes=[
            pltpu.SMEM(seq_lens.shape, jnp.int32),
            pltpu.VMEM(seq_lens.shape, jnp.int32),
            pltpu.VMEM(g_attn.shape, jnp.bfloat16),
            pltpu.VMEM(hidden_in.shape, jnp.bfloat16),
            pltpu.VMEM((hidden_in.shape[1], w_q.shape[1] + 2 * width), jnp.bfloat16),
            pltpu.VMEM((rows // 128, 2 * width, 128), jnp.bfloat16),
            pltpu.VMEM((rows * 8, width), jnp.float32),
            pltpu.VMEM((BLOCK * 8, width), jnp.float32),
            pltpu.VMEM((SLOTS, BLOCK, width, slots), jnp.bfloat16),
            pltpu.VMEM((SLOTS, BLOCK, width, slots), jnp.bfloat16),
            dma((7,)), dma((SLOTS,)), dma((SLOTS,)), dma((SLOTS,)), dma((SLOTS,)),
        ],
        compiler_params=pltpu.CompilerParams(vmem_limit_bytes=26 << 20),
        cost_estimate=pl.CostEstimate(flops=10**9, bytes_accessed=70 * 10**6, transcendentals=0),
        name="attention",
    )(*(pinned(a) for a in (seq_lens, g_attn, hidden_in, w_q, w_k, w_v, k_t, v_t)))


def expert_kernel(o_in, chosen, gain, router, hid, wo_own, wo_peer, w_gate, w_up, w_down, out,
                  wo_pair, wo_pair_far, o_full, w_in, w_dn, x1, h2, gates, z, acc, from_pair, chip_sum, from_far,
                  wi_sem, wd_sem, wo_snd, wo_rcv, o_snd, o_rcv, a_snd, a_rcv, b_snd, b_rcv, c_snd, c_rcv):
    experts, dim, part = w_gate.shape
    rows = hid.shape[0]
    o_rows = rows // 2
    block = rows // PARTS
    cols = dim // CHUNKS
    groups = experts // GROUP
    me = lax.axis_index("tp")
    core, chip = lax.rem(me, 2), lax.div(me, 2)
    pair, far = me + 1 - 2 * core, me + 2 - 4 * chip
    pair_far = far + 1 - 2 * core

    def remote(src, dst, send, recv, to):
        return pltpu.make_async_remote_copy(src_ref=src, dst_ref=dst, send_sem=send, recv_sem=recv,
                                            device_id={"tp": to}, device_id_type=pl.DeviceIdType.MESH)

    def load_in(g):
        sl = pl.ds(g * GROUP, GROUP)
        return (pltpu.make_async_copy(w_gate.at[sl], w_in.at[sl, :, 0:part], wi_sem.at[0, g]),
                pltpu.make_async_copy(w_up.at[sl], w_in.at[sl, :, part:2 * part], wi_sem.at[1, g]))

    def load_down(g):
        sl = pl.ds(g * (w_dn.shape[0] // 4), w_dn.shape[0] // 4)
        return pltpu.make_async_copy(w_down.at[sl], w_dn.at[sl], wd_sem.at[g])

    barrier = pltpu.get_barrier_semaphore()
    for peer in (pair, far):
        pl.semaphore_signal(barrier, inc=1, device_id={"tp": peer}, device_id_type=pl.DeviceIdType.MESH)
    for g in range(groups):
        for copy in load_in(g):
            copy.start()
    for g in range(4):
        load_down(g).start()
    pl.semaphore_wait(barrier, 2)

    def o_block(owner, h, kind, to):
        at = pl.ds(h * o_rows, o_rows)
        src = o_in.at[at] if kind < 2 else o_full.at[owner, at]
        return remote(src, o_full.at[owner, at], o_snd.at[kind, h], o_rcv.at[kind, h], to)

    sends = []

    def go(copy):
        copy.start()
        sends.append(copy)

    wo_copies = [remote(wo_own, wo_pair, wo_snd.at[0], wo_rcv.at[0], pair),
                 remote(wo_peer, wo_pair_far, wo_snd.at[1], wo_rcv.at[1], pair)]
    for h in range(2):
        go(o_block(me, h, 0, far))
    for h in range(2):
        go(o_block(me, h, 1, pair))
    for copy in wo_copies:
        go(copy)

    def relay_o(h):
        o_block(far, h, 0, far).wait_recv()
        go(o_block(far, h, 2, pair))

    def mid(h):
        o_block(pair, h, 1, pair).wait_recv()
        o_block(pair_far, h, 2, pair).wait_recv()
        at = pl.ds(h * o_rows, o_rows)
        total = hid[at, :].astype(jnp.float32)
        for part_o, part_w in ((o_in.at[at], wo_own), (o_full.at[far, at], wo_peer),
                               (o_full.at[pair, at], wo_pair), (o_full.at[pair_far, at], wo_pair_far)):
            total = total + jnp.dot(part_o[...], part_w[...], preferred_element_type=jnp.float32)
        x1[at, :] = total.astype(jnp.bfloat16)

    def routed(at, size):
        h2[at:at + size, :] = normed(x1[at:at + size, :].astype(jnp.float32), gain[...].astype(jnp.float32))
        logits = lax.dot_general(router[...], h2[at:at + size, :], (((1,), (1,)), ((), ())), preferred_element_type=jnp.float32)
        expert_id = lax.broadcasted_iota(jnp.int32, logits.shape, 0)
        picks = chosen[:, at:at + size]
        hit = expert_id == picks[0:1]
        for k in range(1, picks.shape[0]):
            hit = jnp.logical_or(hit, expert_id == picks[k:k + 1])
        shown = jnp.where(hit, logits, MASK_FILL)
        e = jnp.where(hit, jnp.exp(shown - jnp.max(shown, axis=0, keepdims=True)), 0.0)
        g = e / jnp.sum(e, axis=0, keepdims=True)
        gates[at:at + size, :] = jnp.concatenate([g, jnp.zeros((128 - experts, size), jnp.float32)], axis=0).T

    lane = lax.broadcasted_iota(jnp.int32, (block, 128), 1)

    def inner(p, lo, hi):
        def several(i, carry):
            for k in range(UNROLL):
                if p == 0 and k % GROUP == 0:
                    for copy in load_in(i * (UNROLL // GROUP) + k // GROUP):
                        copy.wait()
                e = i * UNROLL + k
                both = jnp.dot(h2[p * block:(p + 1) * block, :], w_in[e], preferred_element_type=jnp.float32)
                gate, up = both[:, :part], both[:, part:]
                weight = jnp.sum(jnp.where(lane == e, gates[p * block:(p + 1) * block, :], 0.0), axis=1, keepdims=True)
                act = weight * (gate / (1.0 + jnp.exp(-gate))) * up
                z[:, pl.ds(pl.multiple_of(e * part, part), part)] = act.astype(jnp.bfloat16)
            return carry
        lax.fori_loop(lo // UNROLL, hi // UNROLL, several, 0)

    def down(p, c):
        acc[p, c] = jnp.dot(z[...], w_dn[:, c * cols:(c + 1) * cols], preferred_element_type=jnp.float32)
        go(pair_copy(p, c))

    def direct(p, c):
        return p * CHUNKS + c >= PARTS * CHUNKS - DIRECT

    def pair_copy(p, c):
        return remote(acc.at[p, c, pl.ds((1 - core) * (block // 2), block // 2)], from_pair.at[p, c], a_snd.at[p, c], a_rcv.at[p, c], pair)

    def far_copy(p, c):
        if direct(p, c):
            return remote(chip_sum.at[p, c], from_far.at[p, c], b_snd.at[p, c], b_rcv.at[p, c], far)
        size = block // 4
        return remote(chip_sum.at[p, c, pl.ds((1 - chip) * size, size)], from_far.at[p, c, 0:size], b_snd.at[p, c], b_rcv.at[p, c], far)

    def out_copy(p, c, kind, of_core, of_chip, to):
        if direct(p, c):
            at = pl.ds(p * block + of_core * (block // 2), block // 2)
        else:
            at = pl.ds(p * block + of_core * (block // 2) + of_chip * (block // 4), block // 4)
        ref = out.at[at, c * cols:(c + 1) * cols]
        return remote(ref, ref, c_snd.at[kind, p, c], c_rcv.at[kind, p, c], to)

    def stage_b(p, c):
        pair_copy(p, c).wait_recv()
        chip_sum[p, c] = acc[p, c, pl.ds(core * (block // 2), block // 2)] + from_pair[p, c]
        go(far_copy(p, c))

    def stage_c(p, c):
        far_copy(p, c).wait_recv()
        cut = slice(c * cols, (c + 1) * cols)
        base = p * block + core * (block // 2)
        if direct(p, c):
            at = pl.ds(base, block // 2)
            total = chip_sum[p, c] + from_far[p, c]
        else:
            at = pl.ds(base + chip * (block // 4), block // 4)
            total = chip_sum[p, c, pl.ds(chip * (block // 4), block // 4)] + from_far[p, c, 0:block // 4]
        out[at, cut] = (x1[at, cut].astype(jnp.float32) + total).astype(jnp.bfloat16)
        if not direct(p, c):
            go(out_copy(p, c, 0, core, chip, far))
        go(out_copy(p, c, 1, core, chip, pair))

    def stage_d(p, c):
        if not direct(p, c):
            out_copy(p, c, 0, core, 1 - chip, far).wait_recv()
            go(out_copy(p, c, 2, core, 1 - chip, pair))

    def stage_e(p, c):
        out_copy(p, c, 1, 1 - core, chip, pair).wait_recv()
        if not direct(p, c):
            out_copy(p, c, 2, 1 - core, 1 - chip, pair).wait_recv()

    relay_o(0)
    for copy in wo_copies:
        copy.wait_recv()
    mid(0)
    if PARTS == 2:
        routed(0, block)
    relay_o(1)
    units = [(p, c) for p in range(PARTS) for c in range(CHUNKS)]
    if PARTS == 1:
        mid(1)
        routed(0, o_rows)
        routed(o_rows, o_rows)
        inner(0, 0, experts)
        for g in range(4):
            load_down(g).wait()
        for c in range(CHUNKS):
            down(0, c)
            if c >= 2:
                stage_b(0, c - 2)
        for c in range(max(CHUNKS - 2, 0), CHUNKS):
            stage_b(0, c)
        rest = units
    else:
        inner(0, 0, experts)
        for g in range(4):
            load_down(g).wait()
        for c in range(CHUNKS):
            down(0, c)
        mid(1)
        routed(block, block)
        for c in range(CHUNKS):
            stage_b(0, c)
        inner(1, 0, experts)
        for c in range(CHUNKS):
            down(1, c)
        for c in range(CHUNKS):
            stage_c(0, c)
        for c in range(CHUNKS):
            stage_b(1, c)
        rest = [(1, c) for c in range(CHUNKS)]
        for c in range(CHUNKS):
            stage_d(0, c)
    for unit in rest:
        stage_c(*unit)
    for unit in rest:
        stage_d(*unit)
    for unit in units:
        stage_e(*unit)
    for copy in sends:
        copy.wait_send()


def expert_call(o, hidden_in, chosen_t, g_moe, router_t, w_o, wo_peer, w_gate, w_up, w_down):
    rows, dim = hidden_in.shape
    experts, _, part = w_gate.shape
    block, cols = rows // PARTS, dim // CHUNKS
    any_spec = pl.BlockSpec(memory_space=pltpu.HBM)
    vmem = pl.BlockSpec(memory_space=pltpu.VMEM)
    dma = pltpu.SemaphoreType.DMA
    bf, f32 = jnp.bfloat16, jnp.float32
    return pl.pallas_call(
        expert_kernel,
        out_shape=jax.ShapeDtypeStruct((rows, dim), bf),
        in_specs=[vmem] * 7 + [any_spec] * 3,
        out_specs=vmem,
        scratch_shapes=[
            pltpu.VMEM(w_o.shape, bf),
            pltpu.VMEM(w_o.shape, bf),
            pltpu.VMEM((4,) + o.shape, bf),
            pltpu.VMEM((experts, dim, 2 * part), bf),
            pltpu.VMEM((experts * part, dim), bf),
            pltpu.VMEM((rows, dim), bf),
            pltpu.VMEM((rows, dim), bf),
            pltpu.VMEM((rows, 128), f32),
            pltpu.VMEM((block, experts * part), bf),
            pltpu.VMEM((PARTS, CHUNKS, block, cols), f32),
            pltpu.VMEM((PARTS, CHUNKS, block // 2, cols), f32),
            pltpu.VMEM((PARTS, CHUNKS, block // 2, cols), f32),
            pltpu.VMEM((PARTS, CHUNKS, block // 2, cols), f32),
            dma((2, experts // GROUP)), dma((4,)), dma((2,)), dma((2,)), dma((3, 2)), dma((3, 2)),
            dma((PARTS, CHUNKS)), dma((PARTS, CHUNKS)), dma((PARTS, CHUNKS)), dma((PARTS, CHUNKS)),
            dma((3, PARTS, CHUNKS)), dma((3, PARTS, CHUNKS)),
        ],
        compiler_params=pltpu.CompilerParams(collective_id=0, has_side_effects=True, vmem_limit_bytes=40 << 20),
        cost_estimate=pl.CostEstimate(flops=7 * 10**9, bytes_accessed=28 * 10**6, transcendentals=0),
        name="experts",
    )(o, chosen_t, g_moe, router_t, hidden_in, w_o, wo_peer, *(pinned(w) for w in (w_gate, w_up, w_down.reshape(experts * part, dim))))


def solution(mesh):
    cache_spec = P("dp", None, "tp", None)
    in_specs = (P("dp", None), cache_spec, cache_spec, P("dp"), P("dp", None), P(None), P(None, "tp"), P(None, "tp"), P(None, "tp"), P("tp", None), P(None), P(None, None), P(None, None, "tp"), P(None, None, "tp"), P(None, "tp", None))
    out_specs = (P("dp", None), cache_spec, cache_spec)

    def layer_shard(hidden_in, k_cache, v_cache, seq_lens, chosen_experts, g_attn, w_q, w_k, w_v, w_o, g_moe, w_router, w_gate, w_up, w_down):
        rows, slots, kvh, hd = k_cache.shape
        as_t = lambda c: c.transpose(0, 2, 3, 1).reshape(rows, kvh * hd, slots)
        back = lambda c: c.reshape(rows, kvh, hd, slots).transpose(0, 3, 1, 2)
        wo_peer = lax.ppermute(w_o, "tp", [(0, 2), (1, 3), (2, 0), (3, 1)])
        o, k_n, v_n = attention_call(hidden_in, as_t(k_cache), as_t(v_cache), seq_lens, g_attn, w_q, w_k, w_v)
        hidden_out = expert_call(o, hidden_in, chosen_experts.T, g_moe, w_router.T, w_o, wo_peer, w_gate, w_up, w_down)
        return hidden_out, back(k_n), back(v_n)

    return jax.shard_map(layer_shard, mesh=mesh, in_specs=in_specs, out_specs=out_specs, check_vma=False)
```

time: 73.4 us -> 59.8 us (0.81)
  Pallas kernels: 63.9 us -> 54.9 us
  local copies, waits for them, and re-layouts: 5.21 us -> 0.81 us
    pallas_call x1, Pallas kernels: 35.4 us -> 28.1 us  [expert_call(): pl.pallas_call(expert_kernel, out_shape=jax.ShapeDtypeStruct((rows, dim),...]
    reshape x2 -> x0, local copies, waits for them, and re-layouts: 2.56 us -> none  [the longest x1 1.28 us: expert_call(): g_moe.reshape(1, -1)]
    unnamed x3 -> x11, local copies, waits for them, and re-layouts: 2.66 us -> 0.81 us
    pallas_call x1, Pallas kernels: 28.5 us -> 26.8 us  [attention_call(): pl.pallas_call(attention_kernel, out_shape=(jax.ShapeDtypeStruct((rows, w...]
  transfers between devices with their start and end apart: 1 -> 1, of which waited for: 0 -> 0; matrix products, arithmetic and copies ran while one was open for 3% -> 0% of each run, Pallas kernels for 39% -> 45%
where the time goes in v2:
time: 59.8 us; the launch traced here: 59.7 us
  Pallas kernels  54.9 us (92%)
  starting transfers between devices  3.36 us (6%)
  local copies, waits for them, and re-layouts  0.81 us (1%)
  between operations  0.71 us (1%)
    pallas_call x1, Pallas kernels, expert_call(): pl.pallas_call(expert_kernel, out_shape=jax.ShapeDtypeStruct((rows, dim),...  28.1 us
    pallas_call x1, Pallas kernels, attention_call(): pl.pallas_call(attention_kernel, out_shape=(jax.ShapeDtypeStruct((rows, w...  26.8 us
    ppermute x1, starting transfers between devices, layer_shard(): wo_peer = lax.ppermute(w_o, 'tp', [(0, 2), (1, 3), (2, 0), (3, 1)])  3.36 us
  transfers between devices with their start and end apart: 1, of which 0 were waited for; matrix products, arithmetic and copies ran while one was open for 0% of the time, Pallas kernels for 45%

profile of v2, /device:TPU:0, one launch (start us, length us, event | category | flops | bytes accessed | tf_op | source)
XLA Modules:
  0.0 59.7 jit_solution(13863034806865163747)
XLA Ops:
  0.6 3.4 %collective-permute-start = (bf16[256,1024]{1,0:T(8,128)(2,1)}, bf16[256,1024]{1,0:T(8,128)(2,1)S(1)}, u32[]{:S(2)}, u32[]{:S(2)}) collective-permute-start(bf16[256,1024]{1,0:T(8,128)(2,1)} %wo_own.1), channel_id=1, source_target_pairs={{0,2},{1,3},{2,0},{3,1},{4,6},{5,7},{6,4},{7,5}} | collective-permute-start | bytes 1572872 | tf_op jit(solution)/shard_map/ppermute | solution.py:438
  4.0 0.0 copy-start
  4.0 0.0 copy-start.1
  4.0 0.0 copy-start.2
  4.0 0.0 copy-start.3
  4.0 0.0 copy-start.4
  4.0 26.8 %attention.1 = (bf16[256,256]{1,0:T(8,128)(2,1)S(1)}, bf16[256,128,256]{2,1,0:T(8,128)(2,1)}, bf16[256,128,256]{2,1,0:T(8,128)(2,1)}) custom-call(s32[256]{0:T(256)} %seq_lens.1, bf16[1024]{0:T(1024)(128)(2,1)} %g_attn.1, bf16[256,1024]{1,0:T(8,128)(2,1)} %hid.1, bf16[1024,256]{1,0:T(8,128)(2,1)} %w_q.1, bf16[1024,128]{1,0:T(8,128)(2,1)} %w_k.1, ...), custom_call_target="tpu_custom_call" | custom-call | flops 1000000000 | bytes 70000000 | tf_op jit(solution)/shard_map/attention/pallas_call | solution.py:161
  30.8 0.0 collective-permute-done.wo_peer
  30.8 0.0 copy-done
  30.8 0.0 copy-done.1
  30.8 0.0 copy-done.2
  30.9 0.0 copy-done.3
  30.9 0.0 copy-done.4
  30.9 28.1 %experts.1 = bf16[256,1024]{1,0:T(8,128)(2,1)S(1)} custom-call(bf16[256,256]{1,0:T(8,128)(2,1)S(1)} %get-tuple-element.6.o_in, s32[8,256]{1,0:T(8,128)S(1)} %bitcast.16, bf16[1024]{0:T(1024)(128)(2,1)S(1)} %copy-done.4, bf16[32,1024]{1,0:T(8,128)(2,1)S(1)} %bitcast.15, bf16[256,1024]{1,0:T(8,128)(2,1)S(1)} %copy-done, bf16[256,1024]{1,0:T(8,128)(2,1)S(1)} %copy-done.1, ...), custom_call_target="tpu_custom_call" | custom-call | flops 7000000000 | bytes 28000000 | tf_op jit(solution)/shard_map/experts/pallas_call | solution.py:400
  58.9 0.8 %copy.19 = bf16[256,1024]{1,0:T(8,128)(2,1)} copy(bf16[256,1024]{1,0:T(8,128)(2,1)S(1)} %experts.1) | data formatting | bytes 1048576
Async XLA Ops:
  0.6 30.2 %collective-permute-start = (bf16[256,1024]{1,0:T(8,128)(2,1)}, bf16[256,1024]{1,0:T(8,128)(2,1)S(1)}, u32[]{:S(2)}, u32[]{:S(2)}) collective-permute-start(bf16[256,1024]{1,0:T(8,128)(2,1)} %wo_own.1), channel_id=1, source_target_pairs={{0,2},{1,3},{2,0},{3,1},{4,6},{5,7},{6,4},{7,5}} | collective-permute-start | bytes 1572872 | tf_op jit(solution)/shard_map/ppermute | solution.py:438
  4.0 26.8 %copy-start = (bf16[256,1024]{1,0:T(8,128)(2,1)S(1)}, bf16[256,1024]{1,0:T(8,128)(2,1)}, u32[]{:S(2)}) copy-start(bf16[256,1024]{1,0:T(8,128)(2,1)} %hid.1) | copy-start | bytes 1572868
  4.0 26.8 %copy-start.1 = (bf16[256,1024]{1,0:T(8,128)(2,1)S(1)}, bf16[256,1024]{1,0:T(8,128)(2,1)}, u32[]{:S(2)}) copy-start(bf16[256,1024]{1,0:T(8,128)(2,1)} %wo_own.1) | copy-start | bytes 1572868
  4.0 26.8 %copy-start.2 = (bf16[1024,32]{0,1:T(8,128)(2,1)S(1)}, bf16[1024,32]{0,1:T(8,128)(2,1)}, u32[]{:S(2)}) copy-start(bf16[1024,32]{0,1:T(8,128)(2,1)} %param.26) | copy-start | bytes 196612
  4.0 26.9 %copy-start.3 = (s32[256,8]{0,1:T(8,128)S(1)}, s32[256,8]{0,1:T(8,128)}, u32[]{:S(2)}) copy-start(s32[256,8]{0,1:T(8,128)} %param.19) | copy-start | bytes 24580
  4.0 26.9 %copy-start.4 = (bf16[1024]{0:T(1024)(128)(2,1)S(1)}, bf16[1024]{0:T(1024)(128)(2,1)}, u32[]{:S(2)}) copy-start(bf16[1024]{0:T(1024)(128)(2,1)} %gain.1) | copy-start | bytes 6148

commit v3 on v2

--- a/solution.py
+++ b/solution.py
@@ -11,12 +11,13 @@
 MASK_FILL = -1e30
 BLOCK = 16
 SLOTS = 8
-AHEAD = 4
+AHEAD = 2
+FIRST = 2
 GROUP = 4
-UNROLL = 8
+UNROLL = 16
 PARTS = 2
 CHUNKS = 2
-DIRECT = 0
+DIRECT = 1
 
 
 def pinned(array):
@@ -54,7 +55,7 @@
              pltpu.make_async_copy(g_attn, gain, w_sem.at[6])]
     for copy in loads:
         copy.start()
-    for i in range(SLOTS):
+    for i in range(FIRST):
         for copy in read(i, i):
             copy.start()
     loads[4].wait()
@@ -63,6 +64,9 @@
     cos_t, sin_t = jnp.cos(angles), jnp.sin(angles)
     for copy in loads[:4] + loads[5:]:
         copy.wait()
+    for i in range(FIRST, SLOTS):
+        for copy in read(i, i):
+            copy.start()
     h = normed(hid[...].astype(jnp.float32), gain[...].astype(jnp.float32))
     qkv_t = jnp.dot(h, wqkv[...], preferred_element_type=jnp.float32).T
 
@@ -87,7 +91,7 @@
         q_rows[pl.ds(r, rows, stride=8), :] = jnp.zeros((rows, width), jnp.float32)
 
     slot_id = lax.broadcasted_iota(jnp.int32, (8, slots), 1)
-    slot_bf = lax.broadcasted_iota(jnp.int32, (width, slots), 1).astype(jnp.float32).astype(jnp.bfloat16)
+    slot_bf = lax.broadcasted_iota(jnp.int32, (width, 128), 1).astype(jnp.float32).astype(jnp.bfloat16)
 
     row_id = lax.broadcasted_iota(jnp.int32, (128, 256), 0) - lax.div(lax.broadcasted_iota(jnp.int32, (128, 256), 1), 128)
     row_bf = row_id.astype(jnp.float32).astype(jnp.bfloat16)
@@ -108,11 +112,10 @@
         places = [seq_s[i * BLOCK + j] for j in range(BLOCK)]
 
         def updated(buf, j, at):
-            col = jnp.concatenate([cols[j][at:at + width]] * (slots // 128), axis=1)
-            here = slot_bf == places[j].astype(jnp.float32).astype(jnp.bfloat16)
-            new = jnp.where(here, col, buf[slot, j])
-            buf[slot, j] = new
-            return new
+            side = pl.ds(pl.multiple_of(lax.div(places[j], 128) * 128, 128), 128)
+            here = slot_bf == lax.rem(places[j], 128).astype(jnp.float32).astype(jnp.bfloat16)
+            buf[slot, j, :, side] = jnp.where(here, cols[j][at:at + width], buf[slot, j, :, side])
+            return buf[slot, j]
 
         scores = []
         for j in range(BLOCK):
@@ -215,8 +218,6 @@
     for g in range(groups):
         for copy in load_in(g):
             copy.start()
-    for g in range(4):
-        load_down(g).start()
     pl.semaphore_wait(barrier, 2)
 
     def o_block(owner, h, kind, to):
@@ -338,6 +339,8 @@
             out_copy(p, c, 2, 1 - core, 1 - chip, pair).wait_recv()
 
     relay_o(0)
+    for g in range(4):
+        load_down(g).start()
     for copy in wo_copies:
         copy.wait_recv()
     mid(0)
@@ -372,9 +375,11 @@
         inner(1, 0, experts)
         for c in range(CHUNKS):
             down(1, c)
-        for c in range(CHUNKS):
-            stage_c(0, c)
-        for c in range(CHUNKS):
+            if c < CHUNKS - 1:
+                stage_c(0, c)
+        stage_b(1, 0)
+        stage_c(0, CHUNKS - 1)
+        for c in range(1, CHUNKS):
             stage_b(1, c)
         rest = [(1, c) for c in range(CHUNKS)]
         for c in range(CHUNKS):

time: 59.8 us -> 54.6 us (0.913)
  Pallas kernels: 54.9 us -> 49.6 us
    pallas_call x1, Pallas kernels: 26.8 us -> 23.5 us  [attention_call(): pl.pallas_call(attention_kernel, out_shape=(jax.ShapeDtypeStruct((rows, w...]
    pallas_call x1, Pallas kernels: 28.1 us -> 26.1 us  [expert_call(): pl.pallas_call(expert_kernel, out_shape=jax.ShapeDtypeStruct((rows, dim),...]
  transfers between devices with their start and end apart: 1 -> 1, of which waited for: 0 -> 0; matrix products, arithmetic and copies ran while one was open for 0% -> 0% of each run, Pallas kernels for 45% -> 43%
where the time goes in v3:
time: 54.6 us; the launch traced here: 54.5 us
  Pallas kernels  49.6 us (91%)
  starting transfers between devices  3.36 us (6%)
  local copies, waits for them, and re-layouts  0.81 us (1%)
  between operations  0.71 us (1%)
    pallas_call x1, Pallas kernels, expert_call(): pl.pallas_call(expert_kernel, out_shape=jax.ShapeDtypeStruct((rows, dim),...  26.1 us
    pallas_call x1, Pallas kernels, attention_call(): pl.pallas_call(attention_kernel, out_shape=(jax.ShapeDtypeStruct((rows, w...  23.5 us
    ppermute x1, starting transfers between devices, layer_shard(): wo_peer = lax.ppermute(w_o, 'tp', [(0, 2), (1, 3), (2, 0), (3, 1)])  3.36 us
  transfers between devices with their start and end apart: 1, of which 0 were waited for; matrix products, arithmetic and copies ran while one was open for 0% of the time, Pallas kernels for 43%

profile of v3, /device:TPU:0, one launch (start us, length us, event | category | flops | bytes accessed | tf_op | source)
XLA Modules:
  0.0 54.5 jit_solution(16529929756111556115)
XLA Ops:
  0.6 3.4 %collective-permute-start = (bf16[256,1024]{1,0:T(8,128)(2,1)}, bf16[256,1024]{1,0:T(8,128)(2,1)S(1)}, u32[]{:S(2)}, u32[]{:S(2)}) collective-permute-start(bf16[256,1024]{1,0:T(8,128)(2,1)} %wo_own.1), channel_id=1, source_target_pairs={{0,2},{1,3},{2,0},{3,1},{4,6},{5,7},{6,4},{7,5}} | collective-permute-start | bytes 1572872 | tf_op jit(solution)/shard_map/ppermute | solution.py:443
  4.0 0.0 copy-start
  4.0 0.0 copy-start.1
  4.0 0.0 copy-start.2
  4.0 0.0 copy-start.3
  4.0 0.0 copy-start.4
  4.0 23.5 %attention.1 = (bf16[256,256]{1,0:T(8,128)(2,1)S(1)}, bf16[256,128,256]{2,1,0:T(8,128)(2,1)}, bf16[256,128,256]{2,1,0:T(8,128)(2,1)}) custom-call(s32[256]{0:T(256)} %seq_lens.1, bf16[1024]{0:T(1024)(128)(2,1)} %g_attn.1, bf16[256,1024]{1,0:T(8,128)(2,1)} %hid.1, bf16[1024,256]{1,0:T(8,128)(2,1)} %w_q.1, bf16[1024,128]{1,0:T(8,128)(2,1)} %w_k.1, ...), custom_call_target="tpu_custom_call" | custom-call | flops 1000000000 | bytes 70000000 | tf_op jit(solution)/shard_map/attention/pallas_call | solution.py:164
  27.6 0.0 collective-permute-done.wo_peer
  27.6 0.0 copy-done
  27.6 0.0 copy-done.1
  27.6 0.0 copy-done.2
  27.6 0.0 copy-done.3
  27.6 0.0 copy-done.4
  27.6 26.1 %experts.1 = bf16[256,1024]{1,0:T(8,128)(2,1)S(1)} custom-call(bf16[256,256]{1,0:T(8,128)(2,1)S(1)} %get-tuple-element.6.o_in, s32[8,256]{1,0:T(8,128)S(1)} %bitcast.16, bf16[1024]{0:T(1024)(128)(2,1)S(1)} %copy-done.4, bf16[32,1024]{1,0:T(8,128)(2,1)S(1)} %bitcast.15, bf16[256,1024]{1,0:T(8,128)(2,1)S(1)} %copy-done, bf16[256,1024]{1,0:T(8,128)(2,1)S(1)} %copy-done.1, ...), custom_call_target="tpu_custom_call" | custom-call | flops 7000000000 | bytes 28000000 | tf_op jit(solution)/shard_map/experts/pallas_call | solution.py:405
  53.7 0.8 %copy.19 = bf16[256,1024]{1,0:T(8,128)(2,1)} copy(bf16[256,1024]{1,0:T(8,128)(2,1)S(1)} %experts.1) | data formatting | bytes 1048576
Async XLA Ops:
  0.6 26.9 %collective-permute-start = (bf16[256,1024]{1,0:T(8,128)(2,1)}, bf16[256,1024]{1,0:T(8,128)(2,1)S(1)}, u32[]{:S(2)}, u32[]{:S(2)}) collective-permute-start(bf16[256,1024]{1,0:T(8,128)(2,1)} %wo_own.1), channel_id=1, source_target_pairs={{0,2},{1,3},{2,0},{3,1},{4,6},{5,7},{6,4},{7,5}} | collective-permute-start | bytes 1572872 | tf_op jit(solution)/shard_map/ppermute | solution.py:443
  4.0 23.6 %copy-start = (bf16[256,1024]{1,0:T(8,128)(2,1)S(1)}, bf16[256,1024]{1,0:T(8,128)(2,1)}, u32[]{:S(2)}) copy-start(bf16[256,1024]{1,0:T(8,128)(2,1)} %hid.1) | copy-start | bytes 1572868
  4.0 23.6 %copy-start.1 = (bf16[256,1024]{1,0:T(8,128)(2,1)S(1)}, bf16[256,1024]{1,0:T(8,128)(2,1)}, u32[]{:S(2)}) copy-start(bf16[256,1024]{1,0:T(8,128)(2,1)} %wo_own.1) | copy-start | bytes 1572868
  4.0 23.6 %copy-start.2 = (bf16[1024,32]{0,1:T(8,128)(2,1)S(1)}, bf16[1024,32]{0,1:T(8,128)(2,1)}, u32[]{:S(2)}) copy-start(bf16[1024,32]{0,1:T(8,128)(2,1)} %param.26) | copy-start | bytes 196612
  4.0 23.6 %copy-start.3 = (s32[256,8]{0,1:T(8,128)S(1)}, s32[256,8]{0,1:T(8,128)}, u32[]{:S(2)}) copy-start(s32[256,8]{0,1:T(8,128)} %param.19) | copy-start | bytes 24580
  4.0 23.6 %copy-start.4 = (bf16[1024]{0:T(1024)(128)(2,1)S(1)}, bf16[1024]{0:T(1024)(128)(2,1)}, u32[]{:S(2)}) copy-start(bf16[1024]{0:T(1024)(128)(2,1)} %gain.1) | copy-start | bytes 6148

commit v4 on v3

--- a/solution.py
+++ b/solution.py
@@ -269,20 +269,21 @@
 
     lane = lax.broadcasted_iota(jnp.int32, (block, 128), 1)
 
-    def inner(p, lo, hi):
+    def inner(p, unroll):
         def several(i, carry):
-            for k in range(UNROLL):
-                if p == 0 and k % GROUP == 0:
-                    for copy in load_in(i * (UNROLL // GROUP) + k // GROUP):
+            if p == 0:
+                for k in range(unroll // GROUP):
+                    for copy in load_in(i * (unroll // GROUP) + k):
                         copy.wait()
-                e = i * UNROLL + k
+            for k in range(unroll):
+                e = i * unroll + k
                 both = jnp.dot(h2[p * block:(p + 1) * block, :], w_in[e], preferred_element_type=jnp.float32)
                 gate, up = both[:, :part], both[:, part:]
                 weight = jnp.sum(jnp.where(lane == e, gates[p * block:(p + 1) * block, :], 0.0), axis=1, keepdims=True)
                 act = weight * (gate / (1.0 + jnp.exp(-gate))) * up
                 z[:, pl.ds(pl.multiple_of(e * part, part), part)] = act.astype(jnp.bfloat16)
             return carry
-        lax.fori_loop(lo // UNROLL, hi // UNROLL, several, 0)
+        lax.fori_loop(0, experts // unroll, several, 0)
 
     def down(p, c):
         acc[p, c] = jnp.dot(z[...], w_dn[:, c * cols:(c + 1) * cols], preferred_element_type=jnp.float32)
@@ -352,7 +353,7 @@
         mid(1)
         routed(0, o_rows)
         routed(o_rows, o_rows)
-        inner(0, 0, experts)
+        inner(0, 32)
         for g in range(4):
             load_down(g).wait()
         for c in range(CHUNKS):
@@ -363,7 +364,7 @@
             stage_b(0, c)
         rest = units
     else:
-        inner(0, 0, experts)
+        inner(0, 32)
         for g in range(4):
             load_down(g).wait()
         for c in range(CHUNKS):
@@ -372,7 +373,7 @@
         routed(block, block)
         for c in range(CHUNKS):
             stage_b(0, c)
-        inner(1, 0, experts)
+        inner(1, 32)
         for c in range(CHUNKS):
             down(1, c)
             if c < CHUNKS - 1:

time: 54.6 us -> 53.3 us (0.976)
  Pallas kernels: 49.6 us -> 48.4 us
    pallas_call x1, Pallas kernels: 26.1 us -> 24.8 us  [expert_call(): pl.pallas_call(expert_kernel, out_shape=jax.ShapeDtypeStruct((rows, dim),...]
  transfers between devices with their start and end apart: 1 -> 1, of which waited for: 0 -> 0; matrix products, arithmetic and copies ran while one was open for 0% -> 0% of each run, Pallas kernels for 43% -> 44%
where the time goes in v4:
time: 53.3 us
  Pallas kernels  48.4 us (91%)
  starting transfers between devices  3.36 us (6%)
  local copies, waits for them, and re-layouts  0.81 us (2%)
  between operations  0.71 us (1%)
    pallas_call x1, Pallas kernels, expert_call(): pl.pallas_call(expert_kernel, out_shape=jax.ShapeDtypeStruct((rows, dim),...  24.8 us
    pallas_call x1, Pallas kernels, attention_call(): pl.pallas_call(attention_kernel, out_shape=(jax.ShapeDtypeStruct((rows, w...  23.5 us
    ppermute x1, starting transfers between devices, layer_shard(): wo_peer = lax.ppermute(w_o, 'tp', [(0, 2), (1, 3), (2, 0), (3, 1)])  3.36 us
  transfers between devices with their start and end apart: 1, of which 0 were waited for; matrix products, arithmetic and copies ran while one was open for 0% of the time, Pallas kernels for 44%

profile of v4, /device:TPU:0, one launch (start us, length us, event | category | flops | bytes accessed | tf_op | source)
XLA Modules:
  0.0 53.3 jit_solution(18025418957092516457)
XLA Ops:
  0.6 3.4 %collective-permute-start = (bf16[256,1024]{1,0:T(8,128)(2,1)}, bf16[256,1024]{1,0:T(8,128)(2,1)S(1)}, u32[]{:S(2)}, u32[]{:S(2)}) collective-permute-start(bf16[256,1024]{1,0:T(8,128)(2,1)} %wo_own.1), channel_id=1, source_target_pairs={{0,2},{1,3},{2,0},{3,1},{4,6},{5,7},{6,4},{7,5}} | collective-permute-start | bytes 1572872 | tf_op jit(solution)/shard_map/ppermute | solution.py:444
  4.0 0.0 copy-start
  4.0 0.0 copy-start.1
  4.0 0.0 copy-start.2
  4.0 0.0 copy-start.3
  4.0 0.0 copy-start.4
  4.0 23.5 %attention.1 = (bf16[256,256]{1,0:T(8,128)(2,1)S(1)}, bf16[256,128,256]{2,1,0:T(8,128)(2,1)}, bf16[256,128,256]{2,1,0:T(8,128)(2,1)}) custom-call(s32[256]{0:T(256)} %seq_lens.1, bf16[1024]{0:T(1024)(128)(2,1)} %g_attn.1, bf16[256,1024]{1,0:T(8,128)(2,1)} %hid.1, bf16[1024,256]{1,0:T(8,128)(2,1)} %w_q.1, bf16[1024,128]{1,0:T(8,128)(2,1)} %w_k.1, ...), custom_call_target="tpu_custom_call" | custom-call | flops 1000000000 | bytes 70000000 | tf_op jit(solution)/shard_map/attention/pallas_call | solution.py:164
  27.6 0.0 collective-permute-done.wo_peer
  27.6 0.0 copy-done
  27.6 0.0 copy-done.1
  27.6 0.0 copy-done.2
  27.6 0.0 copy-done.3
  27.6 0.0 copy-done.4
  27.6 24.8 %experts.1 = bf16[256,1024]{1,0:T(8,128)(2,1)S(1)} custom-call(bf16[256,256]{1,0:T(8,128)(2,1)S(1)} %get-tuple-element.6.o_in, s32[8,256]{1,0:T(8,128)S(1)} %bitcast.16, bf16[1024]{0:T(1024)(128)(2,1)S(1)} %copy-done.4, bf16[32,1024]{1,0:T(8,128)(2,1)S(1)} %bitcast.15, bf16[256,1024]{1,0:T(8,128)(2,1)S(1)} %copy-done, bf16[256,1024]{1,0:T(8,128)(2,1)S(1)} %copy-done.1, ...), custom_call_target="tpu_custom_call" | custom-call | flops 7000000000 | bytes 28000000 | tf_op jit(solution)/shard_map/experts/pallas_call | solution.py:406
  52.5 0.8 %copy.19 = bf16[256,1024]{1,0:T(8,128)(2,1)} copy(bf16[256,1024]{1,0:T(8,128)(2,1)S(1)} %experts.1) | data formatting | bytes 1048576
Async XLA Ops:
  0.6 26.9 %collective-permute-start = (bf16[256,1024]{1,0:T(8,128)(2,1)}, bf16[256,1024]{1,0:T(8,128)(2,1)S(1)}, u32[]{:S(2)}, u32[]{:S(2)}) collective-permute-start(bf16[256,1024]{1,0:T(8,128)(2,1)} %wo_own.1), channel_id=1, source_target_pairs={{0,2},{1,3},{2,0},{3,1},{4,6},{5,7},{6,4},{7,5}} | collective-permute-start | bytes 1572872 | tf_op jit(solution)/shard_map/ppermute | solution.py:444
  4.0 23.6 %copy-start = (bf16[256,1024]{1,0:T(8,128)(2,1)S(1)}, bf16[256,1024]{1,0:T(8,128)(2,1)}, u32[]{:S(2)}) copy-start(bf16[256,1024]{1,0:T(8,128)(2,1)} %hid.1) | copy-start | bytes 1572868
  4.0 23.6 %copy-start.1 = (bf16[256,1024]{1,0:T(8,128)(2,1)S(1)}, bf16[256,1024]{1,0:T(8,128)(2,1)}, u32[]{:S(2)}) copy-start(bf16[256,1024]{1,0:T(8,128)(2,1)} %wo_own.1) | copy-start | bytes 1572868
  4.0 23.6 %copy-start.2 = (bf16[1024,32]{0,1:T(8,128)(2,1)S(1)}, bf16[1024,32]{0,1:T(8,128)(2,1)}, u32[]{:S(2)}) copy-start(bf16[1024,32]{0,1:T(8,128)(2,1)} %param.26) | copy-start | bytes 196612
  4.0 23.6 %copy-start.3 = (s32[256,8]{0,1:T(8,128)S(1)}, s32[256,8]{0,1:T(8,128)}, u32[]{:S(2)}) copy-start(s32[256,8]{0,1:T(8,128)} %param.19) | copy-start | bytes 24580
  4.0 23.6 %copy-start.4 = (bf16[1024]{0:T(1024)(128)(2,1)S(1)}, bf16[1024]{0:T(1024)(128)(2,1)}, u32[]{:S(2)}) copy-start(bf16[1024]{0:T(1024)(128)(2,1)} %gain.1) | copy-start | bytes 6148

commit v5 on v4

--- a/solution.py
+++ b/solution.py
@@ -186,7 +186,7 @@
 
 
 def expert_kernel(o_in, chosen, gain, router, hid, wo_own, wo_peer, w_gate, w_up, w_down, out,
-                  wo_pair, wo_pair_far, o_full, w_in, w_dn, x1, h2, gates, z, acc, from_pair, chip_sum, from_far,
+                  wo_pair, wo_pair_far, o_full, begun, w_in, w_dn, x1, h2, gates, z, acc, from_pair, chip_sum, from_far,
                   wi_sem, wd_sem, wo_snd, wo_rcv, o_snd, o_rcv, a_snd, a_rcv, b_snd, b_rcv, c_snd, c_rcv):
     experts, dim, part = w_gate.shape
     rows = hid.shape[0]
@@ -248,11 +248,12 @@
         o_block(pair, h, 1, pair).wait_recv()
         o_block(pair_far, h, 2, pair).wait_recv()
         at = pl.ds(h * o_rows, o_rows)
-        total = hid[at, :].astype(jnp.float32)
-        for part_o, part_w in ((o_in.at[at], wo_own), (o_full.at[far, at], wo_peer),
-                               (o_full.at[pair, at], wo_pair), (o_full.at[pair_far, at], wo_pair_far)):
-            total = total + jnp.dot(part_o[...], part_w[...], preferred_element_type=jnp.float32)
-        x1[at, :] = total.astype(jnp.bfloat16)
+        for c in range(2):
+            cut = slice(c * (dim // 2), (c + 1) * (dim // 2))
+            total = begun[h, c]
+            for owner, part_w in ((far, wo_peer), (pair, wo_pair), (pair_far, wo_pair_far)):
+                total = total + jnp.dot(o_full[owner, at, :], part_w[:, cut], preferred_element_type=jnp.float32)
+            x1[at, cut] = total.astype(jnp.bfloat16)
 
     def routed(at, size):
         h2[at:at + size, :] = normed(x1[at:at + size, :].astype(jnp.float32), gain[...].astype(jnp.float32))
@@ -339,6 +340,11 @@
         if not direct(p, c):
             out_copy(p, c, 2, 1 - core, 1 - chip, pair).wait_recv()
 
+    for h in range(2):
+        at = pl.ds(h * o_rows, o_rows)
+        for c in range(2):
+            cut = slice(c * (dim // 2), (c + 1) * (dim // 2))
+            begun[h, c] = hid[at, cut].astype(jnp.float32) + jnp.dot(o_in[at, :], wo_own[:, cut], preferred_element_type=jnp.float32)
     relay_o(0)
     for g in range(4):
         load_down(g).start()
@@ -412,6 +418,7 @@
             pltpu.VMEM(w_o.shape, bf),
             pltpu.VMEM(w_o.shape, bf),
             pltpu.VMEM((4,) + o.shape, bf),
+            pltpu.VMEM((2, 2, rows // 2, dim // 2), f32),
             pltpu.VMEM((experts, dim, 2 * part), bf),
             pltpu.VMEM((experts * part, dim), bf),
             pltpu.VMEM((rows, dim), bf),

time: 53.3 us -> 53.1 us (level)
  no operation moved by 1% of the time
where the time goes in v5:
time: 53.1 us; the launch traced here: 53 us
  Pallas kernels  48.1 us (91%)
  starting transfers between devices  3.36 us (6%)
  local copies, waits for them, and re-layouts  0.81 us (2%)
  between operations  0.71 us (1%)
    pallas_call x1, Pallas kernels, expert_call(): pl.pallas_call(expert_kernel, out_shape=jax.ShapeDtypeStruct((rows, dim),...  24.6 us
    pallas_call x1, Pallas kernels, attention_call(): pl.pallas_call(attention_kernel, out_shape=(jax.ShapeDtypeStruct((rows, w...  23.5 us
    ppermute x1, starting transfers between devices, layer_shard(): wo_peer = lax.ppermute(w_o, 'tp', [(0, 2), (1, 3), (2, 0), (3, 1)])  3.36 us
  transfers between devices with their start and end apart: 1, of which 0 were waited for; matrix products, arithmetic and copies ran while one was open for 0% of the time, Pallas kernels for 44%

profile of v5, /device:TPU:0, one launch (start us, length us, event | category | flops | bytes accessed | tf_op | source)
XLA Modules:
  0.0 53.0 jit_solution(14308148262442124583)
XLA Ops:
  0.6 3.4 %collective-permute-start = (bf16[256,1024]{1,0:T(8,128)(2,1)}, bf16[256,1024]{1,0:T(8,128)(2,1)S(1)}, u32[]{:S(2)}, u32[]{:S(2)}) collective-permute-start(bf16[256,1024]{1,0:T(8,128)(2,1)} %wo_own.1), channel_id=1, source_target_pairs={{0,2},{1,3},{2,0},{3,1},{4,6},{5,7},{6,4},{7,5}} | collective-permute-start | bytes 1572872 | tf_op jit(solution)/shard_map/ppermute | solution.py:451
  4.0 0.0 copy-start
  4.0 0.0 copy-start.1
  4.0 0.0 copy-start.2
  4.0 0.0 copy-start.3
  4.0 0.0 copy-start.4
  4.0 23.5 %attention.1 = (bf16[256,256]{1,0:T(8,128)(2,1)S(1)}, bf16[256,128,256]{2,1,0:T(8,128)(2,1)}, bf16[256,128,256]{2,1,0:T(8,128)(2,1)}) custom-call(s32[256]{0:T(256)} %seq_lens.1, bf16[1024]{0:T(1024)(128)(2,1)} %g_attn.1, bf16[256,1024]{1,0:T(8,128)(2,1)} %hid.1, bf16[1024,256]{1,0:T(8,128)(2,1)} %w_q.1, bf16[1024,128]{1,0:T(8,128)(2,1)} %w_k.1, ...), custom_call_target="tpu_custom_call" | custom-call | flops 1000000000 | bytes 70000000 | tf_op jit(solution)/shard_map/attention/pallas_call | solution.py:164
  27.6 0.0 collective-permute-done.wo_peer
  27.6 0.0 copy-done
  27.6 0.0 copy-done.1
  27.6 0.0 copy-done.2
  27.6 0.0 copy-done.3
  27.6 0.0 copy-done.4
  27.6 24.6 %experts.1 = bf16[256,1024]{1,0:T(8,128)(2,1)S(1)} custom-call(bf16[256,256]{1,0:T(8,128)(2,1)S(1)} %get-tuple-element.6.o_in, s32[8,256]{1,0:T(8,128)S(1)} %bitcast.16, bf16[1024]{0:T(1024)(128)(2,1)S(1)} %copy-done.4, bf16[32,1024]{1,0:T(8,128)(2,1)S(1)} %bitcast.15, bf16[256,1024]{1,0:T(8,128)(2,1)S(1)} %copy-done, bf16[256,1024]{1,0:T(8,128)(2,1)S(1)} %copy-done.1, ...), custom_call_target="tpu_custom_call" | custom-call | flops 7000000000 | bytes 28000000 | tf_op jit(solution)/shard_map/experts/pallas_call | solution.py:412
  52.2 0.8 %copy.19 = bf16[256,1024]{1,0:T(8,128)(2,1)} copy(bf16[256,1024]{1,0:T(8,128)(2,1)S(1)} %experts.1) | data formatting | bytes 1048576
Async XLA Ops:
  0.6 26.9 %collective-permute-start = (bf16[256,1024]{1,0:T(8,128)(2,1)}, bf16[256,1024]{1,0:T(8,128)(2,1)S(1)}, u32[]{:S(2)}, u32[]{:S(2)}) collective-permute-start(bf16[256,1024]{1,0:T(8,128)(2,1)} %wo_own.1), channel_id=1, source_target_pairs={{0,2},{1,3},{2,0},{3,1},{4,6},{5,7},{6,4},{7,5}} | collective-permute-start | bytes 1572872 | tf_op jit(solution)/shard_map/ppermute | solution.py:451
  4.0 23.6 %copy-start = (bf16[256,1024]{1,0:T(8,128)(2,1)S(1)}, bf16[256,1024]{1,0:T(8,128)(2,1)}, u32[]{:S(2)}) copy-start(bf16[256,1024]{1,0:T(8,128)(2,1)} %hid.1) | copy-start | bytes 1572868
  4.0 23.6 %copy-start.1 = (bf16[256,1024]{1,0:T(8,128)(2,1)S(1)}, bf16[256,1024]{1,0:T(8,128)(2,1)}, u32[]{:S(2)}) copy-start(bf16[256,1024]{1,0:T(8,128)(2,1)} %wo_own.1) | copy-start | bytes 1572868
  4.0 23.6 %copy-start.2 = (bf16[1024,32]{0,1:T(8,128)(2,1)S(1)}, bf16[1024,32]{0,1:T(8,128)(2,1)}, u32[]{:S(2)}) copy-start(bf16[1024,32]{0,1:T(8,128)(2,1)} %param.26) | copy-start | bytes 196612
  4.0 23.6 %copy-start.3 = (s32[256,8]{0,1:T(8,128)S(1)}, s32[256,8]{0,1:T(8,128)}, u32[]{:S(2)}) copy-start(s32[256,8]{0,1:T(8,128)} %param.19) | copy-start | bytes 24580
  4.0 23.6 %copy-start.4 = (bf16[1024]{0:T(1024)(128)(2,1)S(1)}, bf16[1024]{0:T(1024)(128)(2,1)}, u32[]{:S(2)}) copy-start(bf16[1024]{0:T(1024)(128)(2,1)} %gain.1) | copy-start | bytes 6148
